TPU v7x, 256 devices: a whole 4x4x8 slice. The times are simulated.
256 devices in a mesh: line: 8 (over y, x_hi), surf: 32 (over z, x_lo, core).
Axes of the slice: x: 4 (x_hi: 2, x_lo: 2; x = x_hi * 2 + x_lo), y: 4, z: 8, core: 2. Of those that a mesh axis runs over, the one named last changes fastest.
Arguments:
- face_coef: float32 [32, 4096], P('line', 'surf'), may hold values from 0.5 to 2
- face_mix: float32 [32, 17, 17, 4096], P('line', None, None, 'surf'), may hold values from -0.6 to 0.6
- cell_mix: float32 [32, 17, 17, 4096], P('line', None, None, 'surf'), may hold values from -0.6 to 0.6
- time_term: float32 [32, 17, 4096], P('line', None, 'surf'), may hold values from 0.0005 to 1
- couple: float32 [32, 4, 17, 4096], P('line', None, None, 'surf'), may hold values from 0.0005 to 0.05
- rhs: float32 [32, 17, 4096], P('line', None, 'surf'), may hold values from -0.4 to 0.4
- start_delta: float32 [32, 17, 4096], P('line', None, 'surf'), may hold values from -6 to 6
- neighbours: int32 [4, 4096], P(None, 'surf'), may hold values from -1 to 4095, as said below
- wall_type: int32 [4096], P('surf'), may hold values from 0 to 2
Outputs:
- delta: float32 [32, 17, 4096], P('line', None, 'surf')
Inputs may be any that keep to these rules, and one draw needn't show every extreme that they name: `neighbours`: -1 marks a missing neighbour. Entries 0 and 1 of a line are -1 or lines of its own grid block (blocks are the aligned runs of 128 lines). Entry 2 is a line of its own block or one of the last 16 lines of the block before it; entry 3 a line of its own block or one of the first 16 lines of the block after it; blocks follow one another cyclically. A line is the neighbour of its neighbour. `wall_type`: 0 slip wall, 1 isothermal wall, 2 catalytic wall.
All inputs are finite; a program needn't handle non-finite values.
Results may differ from a plain program's by a relative error of at most 0.0003.
Values sent between devices are 32-bit elements; how exact they have to be, the bound alone decides.
No kernel may reach another device: no remote copies, remote signals or barrier semaphores. Data moves between devices by JAX's collectives and lax.ppermute only.
A program may use at most 64 MiB of HBM per device.

v0:
```python
import jax
import jax.numpy as jnp
from jax import lax
from jax.sharding import PartitionSpec as P

COLS = 16
ITERS = 2


wall_levels = (0.5, 4.0, 32.0)


def from_behind(value, axis, steps):
    count = lax.axis_size(axis)
    initial, last = (max(0, -steps), min(count, count - steps))
    return lax.ppermute(value, axis, [(source, source + steps) for source in range(initial, last)])


def in_one_piece(arrays, axis, dim, along):
    both = jnp.concatenate(arrays, axis=along)
    result, at, finished = (lax.all_gather(both, axis, axis=dim, tiled=True), 0, [])
    for a in arrays:
        finished.append(lax.slice_in_dim(result, at, at + a.shape[along], axis=along))
        at += a.shape[along]
    return tuple(finished)


def padded_2(block, sides, width):
    for axis, dim in sides:
        count = lax.axis_size(axis)
        forward = [(i, i + 1) for i in range(count - 1)]
        forward.append((count - 1, 0))
        backward = [(target, source) for source, target in forward]
        low = lax.ppermute(
            lax.slice_in_dim(block, block.shape[dim] - width, None, axis=dim), axis, forward
        )
        high = lax.ppermute(lax.slice_in_dim(block, 0, width, axis=dim), axis, backward)
        block = jnp.concatenate([low, block, high], axis=dim)
    return block


def from_everyone(array, axis):
    peers = lax.axis_size(axis)
    return lax.all_to_all(
        jnp.broadcast_to(array[None], (peers, *array.shape)), axis, 0, 0, tiled=True
    )


def laid_out(pieces, dim):
    pieces = jnp.moveaxis(pieces, 0, dim)
    shape = pieces.shape
    return pieces.reshape(*shape[:dim], shape[dim] * shape[dim + 1], *shape[dim + 2 :])


def gathered_copies(array, axis, dim):
    pieces = from_everyone(array, axis)
    return laid_out(pieces, dim)


def matrix_product(matrix_left, matrix_right):
    return jnp.sum(matrix_left[:, :, None, :] * matrix_right[None, :, :, :], axis=1)


def matrix_vector(matrix_left, vector_right):
    return jnp.sum(matrix_left * vector_right[None, :, :], axis=1)


def invert(matrix):
    width = matrix.shape[0]
    row_ids = jnp.arange(width)[:, None, None]
    working = matrix
    result = jnp.broadcast_to(jnp.eye(width, dtype=jnp.float32)[:, :, None], matrix.shape)
    for pivot_row in range(width):
        pivot = working[pivot_row, pivot_row]
        row_work = working[pivot_row] / pivot
        row_result = result[pivot_row] / pivot
        factors = working[:, pivot_row]
        is_pivot = row_ids == pivot_row
        working = jnp.where(
            is_pivot, row_work[None], working - factors[:, None, :] * row_work[None]
        )
        result = jnp.where(
            is_pivot, row_result[None], result - factors[:, None, :] * row_result[None]
        )
    return result


def on_device(
    face_coef, face_mix, cell_mix, time_term, couple, rhs, start_delta, neighbours, wall_type
):
    cells, width, _, lines = face_mix.shape
    inner_cells = cells - 1
    identity = jnp.eye(width, dtype=jnp.float32)[:, :, None]
    line_place = lax.axis_index("line")
    is_first = (line_place == 0).astype(jnp.float32)
    wall_term = jnp.zeros(wall_type.shape, jnp.float32)
    for wall_kind, wall_value in enumerate(wall_levels):
        wall_term = wall_term + jnp.where(wall_type == wall_kind, wall_value, 0.0).astype(
            jnp.float32
        )
    below_coef, below_mix = from_behind((face_coef[-1], face_mix[-1]), "line", 1)
    coef_below = jnp.concatenate([below_coef[None], face_coef[:-1]], 0)
    mix_below = jnp.concatenate([below_mix[None], face_mix[:-1]], 0)
    coef_diag = (coef_below + face_coef).at[0].add(is_first * wall_term)
    diag_extra = time_term + jnp.sum(couple, axis=1)
    diagonal = (
        identity[None] * diag_extra[:, None]
        + coef_diag[:, None, None] * identity[None]
        + cell_mix
        - jnp.swapaxes(cell_mix, 1, 2)
    )
    lower = -coef_below[:, None, None] * identity[None] - jnp.swapaxes(mix_below, 1, 2)
    upper = -face_coef[:, None, None] * identity[None] + face_mix
    lower_inner = lower[:inner_cells].at[0].set(0.0)
    source_left = jnp.zeros_like(lower_inner).at[0].set(lower[0])
    zero_matrix = jnp.zeros((width, width, lines), jnp.float32)
    zero_vector = jnp.zeros((width, lines), jnp.float32)

    def factor_step(state_prev, inputs):
        coupler_prev, left_prev = state_prev
        block_diag, block_lower, block_upper, block_source = inputs
        inverse = invert(block_diag - matrix_product(block_lower, coupler_prev))
        coupler_now = matrix_product(inverse, block_upper)
        left_now = matrix_product(inverse, block_source - matrix_product(block_lower, left_prev))
        return ((coupler_now, left_now), (inverse, coupler_now, left_now))

    _, (inverses, couplers, forward_left) = lax.scan(
        factor_step,
        (zero_matrix, zero_matrix),
        (diagonal[:inner_cells], lower_inner, upper[:inner_cells], source_left),
    )

    def back_matrix(state_above, inputs):
        left_above, right_above = state_above
        coupler, left_forward = inputs
        left_now = left_forward - matrix_product(coupler, left_above)
        right_now = -matrix_product(coupler, right_above)
        return ((left_now, right_now), (left_now, right_now))

    minus_identity = -jnp.broadcast_to(identity, (width, width, lines))
    _, (left_part, right_part) = lax.scan(
        back_matrix, (zero_matrix, minus_identity), (couplers, forward_left), reverse=True
    )
    left_next, right_next = from_behind((left_part[0], right_part[0]), "line", -1)
    last_lower = lower[-1]
    last_upper = upper[-1]
    red_lower = -matrix_product(last_lower, left_part[-1])
    red_diag = (
        diagonal[-1]
        - matrix_product(last_lower, right_part[-1])
        - matrix_product(last_upper, left_next)
    )
    red_upper = -matrix_product(last_upper, right_next)
    all_lower, all_diag, all_upper = in_one_piece(
        (red_lower[None], red_diag[None], red_upper[None]), "line", 0, 1
    )

    def chain_factor(coupler_prev, inputs):
        block_lower, block_diag, block_upper = inputs
        inverse = invert(block_diag - matrix_product(block_lower, coupler_prev))
        coupler_now = matrix_product(inverse, block_upper)
        return (coupler_now, (inverse, coupler_now))

    _, (chain_inverse, chain_coupler) = lax.scan(
        chain_factor, zero_matrix, (all_lower, all_diag, all_upper)
    )
    surf_place = lax.axis_index("surf")
    line_total = lines * lax.axis_size("surf")
    line_base = surf_place * lines - COLS
    valid = neighbours >= 0
    local_index = jnp.where(valid, (neighbours - line_base) % line_total, 0)
    weights = couple * valid.astype(jnp.float32)[None, :, None, :]

    def vector_forward(solved_prev, inputs):
        inverse, block_lower, source = inputs
        solved_now = matrix_vector(inverse, source - matrix_vector(block_lower, solved_prev))
        return (solved_now, solved_now)

    def vector_back(solved_above, inputs):
        coupler, forward_value = inputs
        solved_now = forward_value - matrix_vector(coupler, solved_above)
        return (solved_now, solved_now)

    previous = start_delta
    for sweep_number in range(ITERS):
        padded = padded_2(previous, (("surf", 2),), COLS)
        neighbour_vals = jnp.take(padded, local_index, axis=2)
        right_side = rhs + jnp.sum(weights * jnp.swapaxes(neighbour_vals, 1, 2), axis=1)
        _, forward_values = lax.scan(
            vector_forward, zero_vector, (inverses, lower_inner, right_side[:inner_cells])
        )
        _, particular = lax.scan(vector_back, zero_vector, (couplers, forward_values), reverse=True)
        start_next = from_behind(particular[0], "line", -1)
        red_right = (
            right_side[-1]
            - matrix_vector(last_lower, particular[-1])
            - matrix_vector(last_upper, start_next)
        )
        all_right = gathered_copies(red_right[None], "line", 0)
        _, chain_forward = lax.scan(
            vector_forward, zero_vector, (chain_inverse, all_lower, all_right)
        )
        _, separators = lax.scan(
            vector_back, zero_vector, (chain_coupler, chain_forward), reverse=True
        )
        own_sep = lax.dynamic_index_in_dim(separators, line_place, 0, keepdims=False)
        below_place = jnp.maximum(line_place - 1, 0)
        left_sep = lax.dynamic_index_in_dim(separators, below_place, 0, keepdims=False) * (
            1.0 - is_first
        )
        interior = particular - jnp.sum(left_part * left_sep[None, None, :, :], axis=2)
        interior = interior - jnp.sum(right_part * own_sep[None, None, :, :], axis=2)
        previous = jnp.concatenate([interior, own_sep[None]], 0)
    return previous


def solution(mesh):
    placed = (
        P("line", "surf"),
        P("line", None, None, "surf"),
        P("line", None, None, "surf"),
        P("line", None, "surf"),
        P("line", None, None, "surf"),
        P("line", None, "surf"),
        P("line", None, "surf"),
        P(None, "surf"),
        P("surf"),
    )
    return jax.shard_map(
        on_device, mesh=mesh, in_specs=placed, out_specs=P("line", None, "surf"), check_vma=False
    )
```

profile of v0, /device:TPU:99, one launch (start us, length us, event | category | flops | bytes accessed | tf_op | source)
XLA Modules:
  0.0 384.5 jit_solution(4843921389497133254)
XLA Ops:
  7.2 3.7 collective-permute-start
  12.2 4.1 %collective-permute-start.1 = (f32[17,17,128]{2,0,1:T(8,128)S(1)}, f32[17,17,128]{2,0,1:T(8,128)S(1)}, u32[]{:S(2)}, u32[]{:S(2)}) collective-permute-start(f32[17,17,128]{2,0,1:T(8,128)S(1)} %bitcast.953), channel_id=1, source_target_pairs={{0,32},{32,64},{64,96},{96,128},{128,160},{160,192},{192,224},{1,3... | collective-permute-start | bytes 443912 | tf_op jit(solution)/shard_map/ppermute | solution.py:16
  21.3 1.8 copy_add_fusion
  26.9 25.5 %while.172 = (s32[]{:T(128)}, f32[17,17,128]{2,1,0:T(8,128)S(1)}, f32[17,17,128]{2,1,0:T(8,128)S(1)}, f32[3,17,17,128]{3,2,1,0:T(8,128)S(1)}, f32[3,17,17,128]{3...) while((s32[]{:T(128)}, f32[17,17,128]{2,1,0:T(8,128)S(1)}, ...), condition=%wide.region_6.7_spmd, body=%wide.region_1.6_spmd.sunk | while | flops 13019928 | bytes 15185637 | solution.py:127
  54.1 8.0 %while.179 = (s32[]{:T(128)}, f32[17,17,128]{2,1,0:T(8,128)}, f32[17,17,128]{2,1,0:T(8,128)S(1)}, f32[3,17,17,128]{3,2,1,0:T(8,128)S(1)}, f32[3,17,17,128]{3,2,1...) while((s32[]{:T(128)}, f32[17,17,128]{2,1,0:T(8,128)}, ...), condition=%wide.region_18.20_spmd.clone, body=%wide.region_15.19_spmd.clone.sunk | while | flops 2589444 | bytes 3029127 | solution.py:141
  67.7 4.7 %collective-permute-done.4 = f32[17,17,128]{2,1,0:T(8,128)S(1)} collective-permute-done((f32[17,17,128]{2,1,0:T(8,128)S(1)}, f32[17,17,128]{2,1,0:T(8,128)S(1)}, u32[]{:S(2)}, u32[]{:S(2)}) %collective-permute-start.4) | collective-permute-done | bytes 148000 | tf_op jit(solution)/shard_map/ppermute | solution.py:16
  72.4 4.5 %collective-permute-done.5 = f32[17,17,128]{2,1,0:T(8,128)S(1)} collective-permute-done((f32[17,17,128]{2,1,0:T(8,128)S(1)}, f32[17,17,128]{2,1,0:T(8,128)S(1)}, u32[]{:S(2)}, u32[]{:S(2)}) %collective-permute-start.5) | collective-permute-done | bytes 148000 | tf_op jit(solution)/shard_map/ppermute | solution.py:16
  80.5 4.9 %collective-permute-start.2 = (f32[4,17,16]{2,0,1:T(4,128)S(1)}, f32[4,17,16]{2,0,1:T(4,128)S(1)}, u32[]{:S(2)}, u32[]{:S(2)}) collective-permute-start(f32[4,17,16]{2,0,1:T(4,128)S(1)} %get-tuple-element.1364), channel_id=1, source_target_pairs={{0,1},{1,2},{2,3},{3,4},{4,5},{5,6},{6,7},{7,8},{8,9},{9,10},{10,1... | collective-permute-start | bytes 13064 | tf_op jit(solution)/shard_map/ppermute | solution.py:34
  86.4 4.4 %collective-permute-done.3 = f32[4,17,16]{2,0,1:T(4,128)S(1)} collective-permute-done((f32[4,17,16]{2,0,1:T(4,128)S(1)}, f32[4,17,16]{2,0,1:T(4,128)S(1)}, u32[]{:S(2)}, u32[]{:S(2)}) %collective-permute-start.3) | collective-permute-done | bytes 4384 | tf_op jit(solution)/shard_map/ppermute | solution.py:37
  91.9 2.5 gather_fusion
  98.2 4.3 %collective-permute-done.6 = f32[17,128]{1,0:T(8,128)S(1)} collective-permute-done((f32[17,128]{1,0:T(8,128)S(1)}, f32[17,128]{1,0:T(8,128)S(1)}, u32[]{:S(2)}, u32[]{:S(2)}) %collective-permute-start.6) | collective-permute-done | bytes 8736 | tf_op jit(solution)/shard_map/ppermute | solution.py:16
  104.2 7.5 %all-to-all-start = ((f32[8,1,17,128]{3,1,2,0:T(1,128)}), f32[8,1,17,128]{3,1,2,0:T(1,128)S(1)}, u32[]{:S(2)}, u32[]{:S(2)}) async-start(f32[8,1,17,128]{3,1,2,0:T(1,128)} %broadcast_in_dim.1231), calls=%async_computation | async-start | bytes 139264 | tf_op jit(solution)/shard_map/all_to_all | solution.py:44
  111.7 6.7 %all-to-all-done = f32[8,1,17,128]{3,1,2,0:T(1,128)S(1)} async-done(((f32[8,1,17,128]{3,1,2,0:T(1,128)}), f32[8,1,17,128]{3,1,2,0:T(1,128)S(1)}, u32[]{:S(2)}, u32[]{:S(2)}) %all-to-all-start) | async-done | bytes 69664 | tf_op jit(solution)/shard_map/all_to_all | solution.py:44
  119.0 37.8 %all-gather.2.cloned.1.call-done = f32[8,51,17,128]{3,1,2,0:T(8,128)} async-done(((f32[1,51,17,128]{3,1,2,0:T(8,128)}), f32[8,51,17,128]{3,1,2,0:T(8,128)}) %all-gather.2.cloned.1.call-update) | async-done | bytes 3551248 | tf_op jit(solution)/shard_map/all_gather | solution.py:21
  156.8 4.8 %fusion.109 = (f32[8,17,17,128]{3,1,2,0:T(8,128)}, f32[8,17,17,128]{3,1,2,0:T(8,128)S(1)}, f32[8,17,17,128]{3,1,2,0:T(8,128)}) fusion(f32[8,51,17,128]{3,1,2,0:T(8,128)} %all-gather.2.cloned.1.call-done), kind=kLoop, calls=%fused_computation.475 | loop fusion | bytes 7102464 | tf_op jit(solution)/shard_map/slice | solution.py:23
  161.9 66.0 %while.174 = (s32[]{:T(128)}, f32[17,17,128]{2,1,0:T(8,128)S(1)}, f32[8,17,17,128]{3,2,1,0:T(8,128)}, f32[8,17,17,128]{3,2,1,0:T(8,128)}, f32[8,17,17,128]{3,1,2...) while((s32[]{:T(128)}, f32[17,17,128]{2,1,0:T(8,128)S(1)}, ...), condition=%wide.region_26.28_spmd, body=%wide.region_23.27_spmd.sunk | while | flops 10541464 | bytes 14122594 | solution.py:164
  185.0 1.6 select_dynamic-update-slice_fusion.5
  229.1 29.1 %while.175 = (s32[]{:T(128)}, f32[17,128]{1,0:T(8,128)}, f32[8,17,128]{2,1,0:T(8,128)}, f32[8,17,17,128]{3,2,1,0:T(8,128)}, f32[8,17,128]{2,1,0:T(8,128)}, /*index=5*/f32[8,17,17,128]{3,2,1,0:T(8,128)S(1)}, s32[]{:T(128)}) while((s32[]{:T(128)}, f32[17,128]{1,0:T(8,128)}, f32[8,17,128]{2,1,0:T(8,128)}, f32[8,17,17,128]{3,2,1,0:T(8,128)}, ...), condition=%wide.region_32.34_spmd, body=%wide.region_29.33_spmd.sunk | while | flops 145794 | bytes 413301 | solution.py:200
  258.8 33.8 %while.180 = (s32[]{:T(128)}, f32[17,128]{1,0:T(8,128)}, f32[8,17,128]{2,1,0:T(8,128)}, f32[8,17,128]{2,1,0:T(8,128)}, f32[8,17,17,128]{3,2,1,0:T(8,128)}, /*index=5*/s32[]{:T(128)}, s32[]{:T(128)}, s32[]{:T(128)}) while((s32[]{:T(128)}, f32[17,128]{1,0:T(8,128)}, f32[8,17,128]{2,1,0:T(8,128)}, f32[8,17,128]{2,1,0:T(8,128)}, ...), condition=%wide.region_35.37_spmd.clone, body=%wide.region_33.36_spmd.clone.sunk | while | flops 78340 | bytes 242295 | solution.py:203
  296.8 4.7 %collective-permute-start.7 = (f32[4,17,16]{2,0,1:T(4,128)}, f32[4,17,16]{2,0,1:T(4,128)}, u32[]{:S(2)}, u32[]{:S(2)}) collective-permute-start(f32[4,17,16]{2,0,1:T(4,128)} %get-tuple-element.1358), channel_id=1, source_target_pairs={{0,1},{1,2},{2,3},{3,4},{4,5},{5,6},{6,7},{7,8},{8,9},{9,10},{10,1... | collective-permute-start | bytes 13064 | tf_op jit(solution)/shard_map/ppermute | solution.py:34
  302.9 4.4 %collective-permute-done.8 = f32[4,17,16]{2,0,1:T(4,128)} collective-permute-done((f32[4,17,16]{2,0,1:T(4,128)}, f32[4,17,16]{2,0,1:T(4,128)}, u32[]{:S(2)}, u32[]{:S(2)}) %collective-permute-start.8) | collective-permute-done | bytes 4384 | tf_op jit(solution)/shard_map/ppermute | solution.py:37
  307.3 1.6 pad_maximum_fusion.2
  308.9 1.8 copy.155
  310.7 3.5 gather_fusion.1
  314.2 2.2 copy.163
  320.1 11.2 %while.176 = (s32[]{:T(128)}, f32[17,128]{1,0:T(8,128)}, f32[3,17,128]{2,1,0:T(8,128)}, f32[3,17,17,128]{3,2,1,0:T(8,128)}, f32[3,17,128]{2,0,1:T(4,128)}, /*index=5*/f32[3,17,17,128]{3,2,1,0:T(8,128)S(1)}, s32[]{:T(128)}) while((s32[]{:T(128)}, f32[17,128]{1,0:T(8,128)}, f32[3,17,128]{2,1,0:T(8,128)}, f32[3,17,17,128]{3,2,1,0:T(8,128)}, ...), condition=%wide.region_42.44_spmd, body=%wide.region_39.43_spmd.sunk | while | flops 145794 | bytes 430709 | solution.py:189
  331.9 9.5 %while.181 = (s32[]{:T(128)}, f32[17,128]{1,0:T(8,128)}, f32[3,17,128]{2,1,0:T(8,128)}, f32[3,17,128]{2,1,0:T(8,128)}, f32[3,17,17,128]{3,2,1,0:T(8,128)S(1)}, /*index=5*/s32[]{:T(128)}, s32[]{:T(128)}, s32[]{:T(128)}) while((s32[]{:T(128)}, f32[17,128]{1,0:T(8,128)}, f32[3,17,128]{2,1,0:T(8,128)}, f32[3,17,128]{2,1,0:T(8,128)}, ...), condition=%wide.region_45.47_spmd.clone, body=%wide.region_43.46_spmd.clone.sunk | while | flops 78340 | bytes 242295 | solution.py:192
  345.2 2.9 collective-permute-done.9
  349.7 3.4 all-to-all-start.1
  353.1 6.6 %all-to-all-done.1 = f32[8,1,17,128]{3,1,2,0:T(1,128)S(1)} async-done(((f32[8,1,17,128]{3,1,2,0:T(1,128)}), f32[8,1,17,128]{3,1,2,0:T(1,128)S(1)}, u32[]{:S(2)}, u32[]{:S(2)}) %all-to-all-start.1) | async-done | bytes 69664 | tf_op jit(solution)/shard_map/all_to_all | solution.py:44
  359.7 8.6 %while.177 = (s32[]{:T(128)}, f32[17,128]{1,0:T(8,128)S(1)}, f32[8,17,128]{2,1,0:T(8,128)S(1)}, f32[8,17,17,128]{3,2,1,0:T(8,128)}, f32[8,17,128]{2,1,0:T(8,128)S(1)}, /*index=5*/f32[8,17,17,128]{3,2,1,0:T(8,128)S(1)}, s32[]{:T(128)}) while((s32[]{:T(128)}, f32[17,128]{1,0:T(8,128)S(1)}, f32[8,17,128]{2,1,0:T(8,128)S(1)}, ...), condition=%wide.region_51.53_spmd, body=%wide.region_48.52_spmd.sunk | while | flops 145794 | bytes 381533 | solution.py:200
  368.4 8.4 %while.182 = (s32[]{:T(128)}, f32[17,128]{1,0:T(8,128)S(1)}, f32[8,17,128]{2,1,0:T(8,128)S(1)}, f32[8,17,128]{2,1,0:T(8,128)S(1)}, f32[8,17,17,128]{3,2,1,0:T(8,128)}, /*index=5*/s32[]{:T(128)}, s32[]{:T(128)}, s32[]{:T(128)}) while((s32[]{:T(128)}, f32[17,128]{1,0:T(8,128)S(1)}, f32[8,17,128]{2,1,0:T(8,128)S(1)}, ...), condition=%wide.region_54.56_spmd.clone, body=%wide.region_52.55_spmd.clone.sunk | while | flops 78340 | bytes 245879 | solution.py:203
  (1549 shorter events, 238.1 us)
Async XLA Ops:
  6.5 150.2 %all-gather.2.cloned.1.call-start = ((), (), s32[]{:S(2)}) async-start(), calls=%async_computation.2 | async-start | bytes 4386816 | tf_op jit(solution)/shard_map/all_gather | solution.py:21
  7.2 12.6 %collective-permute-start = (f32[128]{0:T(128)S(1)}, f32[128]{0:T(128)S(1)}, u32[]{:S(2)}, u32[]{:S(2)}) collective-permute-start(f32[128]{0:T(128)S(1)} %slice_bitcast_fusion.44), channel_id=1, source_target_pairs={{0,32},{32,64},{64,96},{96,128},{128,160},{160,192},{192,224},{1,3... | collective-permute-start | bytes 1544 | tf_op jit(solution)/shard_map/ppermute | solution.py:16
  12.2 9.1 %collective-permute-start.1 = (f32[17,17,128]{2,0,1:T(8,128)S(1)}, f32[17,17,128]{2,0,1:T(8,128)S(1)}, u32[]{:S(2)}, u32[]{:S(2)}) collective-permute-start(f32[17,17,128]{2,0,1:T(8,128)S(1)} %bitcast.953), channel_id=1, source_target_pairs={{0,32},{32,64},{64,96},{96,128},{128,160},{160,192},{192,224},{1,3... | collective-permute-start | bytes 443912 | tf_op jit(solution)/shard_map/ppermute | solution.py:16
  19.8 5.0 %copy-start.19 = (pred[3]{0:T(512)(128)(4,1)S(1)}, pred[3]{0:T(512)(128)(4,1)}, u32[]{:S(2)}) copy-start(pred[3]{0:T(512)(128)(4,1)} %constant.506.clone.1) | copy-start | bytes 13
  23.1 1.0 copy-start.4
  23.1 3.7 copy-start.5
  23.1 3.7 copy-start.6
  62.2 18.2 %copy-start.1 = (f32[3,17,17,128]{3,2,1,0:T(8,128)}, f32[3,17,17,128]{3,2,1,0:T(8,128)S(1)}, u32[]{:S(2)}) copy-start(f32[3,17,17,128]{3,2,1,0:T(8,128)S(1)} %get-tuple-element.821) | copy-start | bytes 1331716
  63.4 16.9 %copy-start.10 = (f32[4,17,128]{2,0,1:T(4,128)S(1)}, f32[4,17,128]{2,0,1:T(4,128)}, u32[]{:S(2)}) copy-start(f32[4,17,128]{2,0,1:T(4,128)} %param.45) | copy-start | bytes 104452
  63.5 21.8 %copy-start.18 = (s32[4,128]{1,0:T(4,128)S(1)}, s32[4,128]{1,0:T(4,128)}, u32[]{:S(2)}) copy-start(s32[4,128]{1,0:T(4,128)} %param.46) | copy-start | bytes 6148
  63.5 8.9 %collective-permute-start.4 = (f32[17,17,128]{2,1,0:T(8,128)S(1)}, f32[17,17,128]{2,1,0:T(8,128)S(1)}, u32[]{:S(2)}, u32[]{:S(2)}) collective-permute-start(f32[17,17,128]{2,1,0:T(8,128)S(1)} %get-tuple-element.1353), channel_id=1, source_target_pairs={{32,0},{64,32},{96,64},{128,96},{160,128},{192,160},{224,192},{33,... | collective-permute-start | bytes 443912 | tf_op jit(solution)/shard_map/ppermute | solution.py:16
  64.8 12.1 %collective-permute-start.5 = (f32[17,17,128]{2,1,0:T(8,128)S(1)}, f32[17,17,128]{2,1,0:T(8,128)S(1)}, u32[]{:S(2)}, u32[]{:S(2)}) collective-permute-start(f32[17,17,128]{2,1,0:T(8,128)S(1)} %get-tuple-element.1351), channel_id=1, source_target_pairs={{32,0},{64,32},{96,64},{128,96},{160,128},{192,160},{224,192},{33,... | collective-permute-start | bytes 443912 | tf_op jit(solution)/shard_map/ppermute | solution.py:16
  67.7 27.0 %copy-start.9 = (f32[4,4,17,128]{3,1,2,0:T(4,128)S(1)}, f32[4,4,17,128]{3,1,2,0:T(4,128)}, u32[]{:S(2)}) copy-start(f32[4,4,17,128]{3,1,2,0:T(4,128)} %param.43) | copy-start | bytes 417796
  78.4 16.5 %copy-start.14 = (f32[4,17,128]{2,0,1:T(4,128)S(1)}, f32[4,17,128]{2,0,1:T(4,128)}, u32[]{:S(2)}) copy-start(f32[4,17,128]{2,0,1:T(4,128)} %param.44) | copy-start | bytes 104452
  80.5 5.9 %collective-permute-start.2 = (f32[4,17,16]{2,0,1:T(4,128)S(1)}, f32[4,17,16]{2,0,1:T(4,128)S(1)}, u32[]{:S(2)}, u32[]{:S(2)}) collective-permute-start(f32[4,17,16]{2,0,1:T(4,128)S(1)} %get-tuple-element.1364), channel_id=1, source_target_pairs={{0,1},{1,2},{2,3},{3,4},{4,5},{5,6},{6,7},{7,8},{8,9},{9,10},{10,1... | collective-permute-start | bytes 13064 | tf_op jit(solution)/shard_map/ppermute | solution.py:34
  85.3 5.5 %collective-permute-start.3 = (f32[4,17,16]{2,0,1:T(4,128)S(1)}, f32[4,17,16]{2,0,1:T(4,128)S(1)}, u32[]{:S(2)}, u32[]{:S(2)}) collective-permute-start(f32[4,17,16]{2,0,1:T(4,128)S(1)} %get-tuple-element.1365), channel_id=1, source_target_pairs={{1,0},{2,1},{3,2},{4,3},{5,4},{6,5},{7,6},{8,7},{9,8},{10,9},{11,1... | collective-permute-start | bytes 13064 | tf_op jit(solution)/shard_map/ppermute | solution.py:37
  85.4 10.1 %copy-start.17 = (pred[4,128]{1,0:T(4,128)(4,1)}, pred[4,128]{1,0:T(4,128)(4,1)S(1)}, u32[]{:S(2)}) copy-start(pred[4,128]{1,0:T(4,128)(4,1)S(1)} %get-tuple-element.1202) | copy-start | bytes 1540
  85.4 10.1 %copy-start.16 = (s32[1024]{0:T(1024)}, s32[1024]{0:T(1024)S(1)}, u32[]{:S(2)}) copy-start(s32[1024]{0:T(1024)S(1)} %pad_clamp_fusion) | copy-start | bytes 12292
  95.4 66.1 %copy-start = (f32[3,17,17,128]{3,2,1,0:T(8,128)}, f32[3,17,17,128]{3,2,1,0:T(8,128)S(1)}, u32[]{:S(2)}) copy-start(f32[3,17,17,128]{3,2,1,0:T(8,128)S(1)} %get-tuple-element.2366) | copy-start | bytes 1331716
  95.9 8.3 %copy-start.12 = (f32[3,17,128]{2,1,0:T(8,128)}, f32[3,17,128]{2,1,0:T(8,128)S(1)}, u32[]{:S(2)}) copy-start(f32[3,17,128]{2,1,0:T(8,128)S(1)} %get-tuple-element.819) | copy-start | bytes 78340
  95.9 6.6 %collective-permute-start.6 = (f32[17,128]{1,0:T(8,128)S(1)}, f32[17,128]{1,0:T(8,128)S(1)}, u32[]{:S(2)}, u32[]{:S(2)}) collective-permute-start(f32[17,128]{1,0:T(8,128)S(1)} %get-tuple-element.1363), channel_id=1, source_target_pairs={{32,0},{64,32},{96,64},{128,96},{160,128},{192,160},{224,192},{33,... | collective-permute-start | bytes 26120 | tf_op jit(solution)/shard_map/ppermute | solution.py:16
  104.2 14.2 %all-to-all-start = ((f32[8,1,17,128]{3,1,2,0:T(1,128)}), f32[8,1,17,128]{3,1,2,0:T(1,128)S(1)}, u32[]{:S(2)}, u32[]{:S(2)}) async-start(f32[8,1,17,128]{3,1,2,0:T(1,128)} %broadcast_in_dim.1231), calls=%async_computation | async-start | bytes 139264 | tf_op jit(solution)/shard_map/all_to_all | solution.py:44
  227.9 65.5 %copy-start.2 = (f32[3,17,17,128]{3,2,1,0:T(8,128)S(1)}, f32[3,17,17,128]{3,2,1,0:T(8,128)}, u32[]{:S(2)}) copy-start(f32[3,17,17,128]{3,2,1,0:T(8,128)} %copy-done.1) | copy-start | bytes 1331716
  293.5 3.3 copy-start.15
  295.5 0.6 copy-start.11
  296.8 6.0 %collective-permute-start.7 = (f32[4,17,16]{2,0,1:T(4,128)}, f32[4,17,16]{2,0,1:T(4,128)}, u32[]{:S(2)}, u32[]{:S(2)}) collective-permute-start(f32[4,17,16]{2,0,1:T(4,128)} %get-tuple-element.1358), channel_id=1, source_target_pairs={{0,1},{1,2},{2,3},{3,4},{4,5},{5,6},{6,7},{7,8},{8,9},{9,10},{10,1... | collective-permute-start | bytes 13064 | tf_op jit(solution)/shard_map/ppermute | solution.py:34
  301.5 5.8 %collective-permute-start.8 = (f32[4,17,16]{2,0,1:T(4,128)}, f32[4,17,16]{2,0,1:T(4,128)}, u32[]{:S(2)}, u32[]{:S(2)}) collective-permute-start(f32[4,17,16]{2,0,1:T(4,128)} %get-tuple-element.1359), channel_id=1, source_target_pairs={{1,0},{2,1},{3,2},{4,3},{5,4},{6,5},{7,6},{8,7},{9,8},{10,9},{11,1... | collective-permute-start | bytes 13064 | tf_op jit(solution)/shard_map/ppermute | solution.py:37
  322.6 0.6 copy-start.8
  331.9 44.9 %copy-start.3 = (f32[3,17,17,128]{3,2,1,0:T(8,128)S(1)}, f32[3,17,17,128]{3,2,1,0:T(8,128)}, u32[]{:S(2)}) copy-start(f32[3,17,17,128]{3,2,1,0:T(8,128)} %get-tuple-element.822) | copy-start | bytes 1331716
  342.1 5.9 %collective-permute-start.9 = (f32[17,128]{1,0:T(8,128)S(1)}, f32[17,128]{1,0:T(8,128)S(1)}, u32[]{:S(2)}, u32[]{:S(2)}) collective-permute-start(f32[17,128]{1,0:T(8,128)S(1)} %get-tuple-element.1361), channel_id=1, source_target_pairs={{32,0},{64,32},{96,64},{128,96},{160,128},{192,160},{224,192},{33,... | collective-permute-start | bytes 26120 | tf_op jit(solution)/shard_map/ppermute | solution.py:16
  343.4 33.6 %copy-start.13 = (f32[3,17,128]{2,1,0:T(8,128)S(1)}, f32[3,17,128]{2,1,0:T(8,128)}, u32[]{:S(2)}) copy-start(f32[3,17,128]{2,1,0:T(8,128)} %get-tuple-element.828) | copy-start | bytes 78340
  349.7 10.0 %all-to-all-start.1 = ((f32[8,1,17,128]{3,1,2,0:T(1,128)}), f32[8,1,17,128]{3,1,2,0:T(1,128)S(1)}, u32[]{:S(2)}, u32[]{:S(2)}) async-start(f32[8,1,17,128]{3,1,2,0:T(1,128)} %broadcast_in_dim.1232), calls=%async_computation.1 | async-start | bytes 139264 | tf_op jit(solution)/shard_map/all_to_all | solution.py:44
  (10 other events, 5.9 us)
Sparse Core Ops, SparseCore 0:
  80.5 76.2 all-gather.1
where the time goes:
time: 390 us; the launch traced here: 385 us
  other arithmetic  181 us (46%)
  waiting for transfers between devices  78.7 us (20%)
  local copies, waits for them, and re-layouts  68.2 us (17%)
  starting transfers between devices  33.3 us (9%)
  between operations  14.1 us (4%)
  loops' own time  9.01 us (2%)
    reduce_sum x70, other arithmetic, matrix_vector(): return jnp.sum(matrix_left * vector_right[None, :, :], axis=1)  47.1 us
    all_gather x1, waiting for transfers between devices, in_one_piece(): lax.all_gather(both, axis, axis=dim, tiled=True)  37.8 us
    select_n x121, other arithmetic, invert(): jnp.where(is_pivot, row_work[None], working - factors[:, None, :] * row_w...  16.7 us
    select_n x77, other arithmetic, invert(): jnp.where(is_pivot, row_result[None], result - factors[:, None, :] * row_...  16.6 us
    ppermute x6, waiting for transfers between devices, from_behind(): lax.ppermute(value, axis, [(source, source + steps) for source in range(i...  16.4 us
    sub x22, other arithmetic, vector_back(): solved_now = forward_value - matrix_vector(coupler, solved_above)  14.5 us
    all_to_all x2, waiting for transfers between devices, from_everyone(): lax.all_to_all(jnp.broadcast_to(array[None], (peers, *array.shape)), axis...  13.3 us
    ppermute x6, starting transfers between devices, from_behind(): lax.ppermute(value, axis, [(source, source + steps) for source in range(i...  13 us
  transfers between devices with their start and end apart: 13, of which 11 were waited for; matrix products, arithmetic and copies ran while one was open for 5% of the time, Pallas kernels for 0%

commit v1 on v0

v1 whole, which is shorter than its diff:
```python
import jax
import jax.numpy as jnp
from jax import lax
from jax.experimental import pallas as pl
from jax.experimental.pallas import tpu as pltpu
from jax.sharding import PartitionSpec as P

COLS = 16
WIDTH = 17
GROUPS = 8
LANES = 128
DROWS = 24 * WIDTH
BROWS = 40 * WIDTH
BELOWROWS = 296
VROWS = 72
MATRIX_GROUPS = 43
TOTALROWS = 64 * (MATRIX_GROUPS + 2)
CELL_AT, TIME_AT, RHS_AT, COUPLE_AT, COEF_AT, RIGHT_AT = 1160, 2320, 2392, 2464, 2736, 2752
WALLS = (0.5, 4.0, 32.0)
FP = jnp.float32


def lane_ids(rows):
    return lax.broadcasted_iota(jnp.int32, (rows, LANES), 1)


def sub_ids(rows):
    return lax.broadcasted_iota(jnp.int32, (rows, LANES), 0)


def swap_blocks(regs):
    lanes = lane_ids(8)
    for k in (1, 2, 4):
        high = (lanes // (COLS * k)) % 2 == 1
        result = list(regs)
        for a in range(8):
            if a & k:
                continue
            b = a | k
            result[a] = jnp.where(high, pltpu.roll(regs[b], COLS * k, 1), regs[a])
            result[b] = jnp.where(high, regs[b], pltpu.roll(regs[a], LANES - COLS * k, 1))
        regs = result
    return regs


def row(ref, at):
    return ref[pl.ds(at, 1), :]


def tile(ref, at):
    return ref[pl.ds(at, 8), :]


def strided(ref, at, stride):
    return ref[pl.ds(at, 8, stride=stride), :]


def along(value, lanes):
    rows = value.shape[0]
    value, lanes = jnp.broadcast_to(value, (8, LANES)), jnp.broadcast_to(lanes, (8, LANES))
    return jnp.take_along_axis(value, lanes, axis=1, mode="promise_in_bounds")[:rows]


def pack_kernel(coef_ref, face_ref, cell_ref, time_ref, couple_ref, rhs_ref, out_ref, stage):
    pieces = []
    for ref in (face_ref, cell_ref, time_ref, rhs_ref, couple_ref, coef_ref):
        rows = ref.size // LANES
        flat = ref if len(ref.shape) == 2 else ref.reshape(rows, LANES)
        for at in range(0, rows - 7, 8):
            pieces.append((flat, at))
        if rows % 8:
            spot = 8 * len([p for p in pieces if p[0] is stage])
            stage[pl.ds(spot, 8), :] = jnp.zeros((8, LANES), FP)
            stage[pl.ds(spot, rows % 8), :] = flat[pl.ds(rows - rows % 8, rows % 8), :]
            pieces.append((stage, spot))
    zeros = jnp.zeros((8, LANES), FP)
    for g in range(MATRIX_GROUPS):
        regs = []
        for w in range(8):
            n = 8 * g + w
            regs.append(tile(*pieces[n]) if n < len(pieces) else zeros)
        regs = swap_blocks(regs)
        for d in range(8):
            out_ref[d, pl.ds(8 * g, 8), :] = regs[d]


def right_kernel(
    start_ref, low_ref, high_ref, index_ref, from_ref, couple_ref, rhs_ref, _, out_ref, stage, sem,
):
    start, low, high, rhs = [ref.reshape(4 * WIDTH, LANES) for ref in (start_ref, low_ref, high_ref, rhs_ref)]
    couple = couple_ref.reshape(16 * WIDTH, LANES)
    ids = sub_ids(8)
    lanes = [jnp.broadcast_to(index_ref[pl.ds(n, 1), :], (8, LANES)) for n in range(4)]
    kinds = [jnp.broadcast_to(from_ref[pl.ds(n, 1), :], (8, LANES)) for n in range(4)]

    def total(load, weight):
        value = load(rhs)
        sources = [load(ref) for ref in (start, low, high)]
        for n in range(4):
            got = jnp.zeros((8, LANES), FP)
            for d, source in enumerate(sources):
                got = jnp.where(kinds[n] == d, along(source, lanes[n]), got)
            value = value + weight(n) * got
        return value

    regs = []
    for c in range(4):
        for h in range(2):
            regs.append(total(
                lambda ref: strided(ref, 32 * h + c, 4),
                lambda n: strided(couple, (17 * c + 8 * h) * 4 + n, 4),
            ))

    def last_weight(n):
        value = jnp.zeros((8, LANES), FP)
        for c in range(4):
            value = jnp.where(ids == 4 + c, row(couple, (17 * c + 16) * 4 + n), value)
        return value

    regs.append(total(lambda ref: tile(ref, 60), last_weight))
    zeros = jnp.zeros((8, LANES), FP)
    for g in range(2):
        part = swap_blocks((regs + [zeros] * 7)[8 * g : 8 * g + 8])
        for d in range(8):
            stage[d, pl.ds(8 * g, 8), :] = part[d]
    copy = pltpu.make_async_copy(stage, out_ref.at[:, pl.ds(8 * MATRIX_GROUPS, 16), :], sem)
    copy.start()
    copy.wait()


def left_at(j):
    return j if j < 16 else 32


def right_at(j):
    return 16 + j if j < 16 else 33


def invert_in_place(refs):
    ids = sub_ids(8)
    for k in range(WIDTH):
        for ref, base in refs:
            pivot = jnp.broadcast_to(1.0 / row(ref, base + 24 * k + k), (8, LANES))
            scaled = [tile(ref, base + 24 * k + 8 * v) * pivot for v in range(3)]
            here = ids == k % 8
            scaled[k // 8] = jnp.where(here, pivot, scaled[k // 8])
            for i in range(WIDTH):
                if i == k:
                    continue
                factor = row(ref, base + 24 * i + k)
                for v in range(3):
                    old = tile(ref, base + 24 * i + 8 * v)
                    if v == k // 8:
                        old = jnp.where(here, 0.0, old)
                    ref[pl.ds(base + 24 * i + 8 * v, 8), :] = old - factor * scaled[v]
            for v in range(3):
                ref[pl.ds(base + 24 * k + 8 * v, 8), :] = scaled[v]


def normalise(inverse, inverse_base, source, source_base, result, result_base):
    def step(i, _):
        at = pl.multiple_of(24 * i, 8)
        sums = [None] * 5
        for j in range(WIDTH):
            factor = row(inverse, inverse_base + at + j)
            for v in range(5):
                term = factor * tile(source, source_base + 40 * j + 8 * v)
                sums[v] = term if j == 0 else sums[v] + term
        to = pl.multiple_of(40 * i, 8)
        for v in range(5):
            result[pl.ds(result_base + to + 8 * v, 8), :] = sums[v]
        return 0

    lax.fori_loop(0, WIDTH, step, 0)


def eliminate(blocks, base, diag, diag_base, low, low_base, high, high_base, new, new_base, new_diag, new_diag_base):
    ids = sub_ids(8)

    def step(i, _):
        at = pl.multiple_of(40 * i, 8)
        first, second = [None] * 5, [None] * 5
        for j in range(WIDTH):
            below = row(blocks, base + at + left_at(j))
            above = row(blocks, base + at + right_at(j))
            for v in range(5):
                term = below * tile(low, low_base + 40 * j + 8 * v)
                first[v] = term if j == 0 else first[v] + term
                term = above * tile(high, high_base + 40 * j + 8 * v)
                second[v] = term if j == 0 else second[v] + term
        for v in range(2):
            new[pl.ds(new_base + at + 8 * v, 8), :] = -first[v]
            new[pl.ds(new_base + at + 16 + 8 * v, 8), :] = -second[2 + v]
        rest = tile(blocks, base + at + 32) - first[4] - second[4]
        rest = jnp.where(ids == 0, -first[4], jnp.where(ids == 1, -second[4], rest))
        new[pl.ds(new_base + at + 32, 8), :] = rest
        to = pl.multiple_of(24 * i, 8)
        for v in range(2):
            new_diag[pl.ds(new_diag_base + to + 8 * v, 8), :] = (
                tile(diag, diag_base + to + 8 * v) - first[2 + v] - second[v]
            )
        new_diag[pl.ds(new_diag_base + to + 16, 8), :] = (
            tile(diag, diag_base + to + 16) - pltpu.roll(first[4], 7, 0) - second[4]
        )
        return 0

    lax.fori_loop(0, WIDTH, step, 0)


def matvec(ref, base, stride, at, value_row):
    sums = [None] * 3
    for j in range(WIDTH):
        value = value_row(j)
        here = at(j)
        for h in range(2):
            term = strided(ref, base + 8 * h * stride + here, stride) * value
            sums[h] = term if j == 0 else sums[h] + term
        term = row(ref, base + 16 * stride + here) * value
        sums[2] = term if j == 0 else sums[2] + term
    return sums


def minus(a, b):
    return [x - y for x, y in zip(a, b)]


def plain(j):
    return j


def vector_of(ref, base, last):
    return [tile(ref, base), tile(ref, base + 8), row(ref, last)]


def put_vector(ref, base, last, value):
    ref[pl.ds(base, 8), :] = value[0]
    ref[pl.ds(base + 8, 8), :] = value[1]
    ref[pl.ds(last, 1), :] = value[2]


def moved(value, steps):
    return [pltpu.roll(x, (COLS * steps) % LANES, 1) for x in value]


class Scratch:
    def __init__(self, ref):
        self.ref, self.next = ref, 0

    def hold(self, value):
        base = 24 * self.next
        self.next += 1
        put_vector(self.ref, base, base + 16, value)
        return lambda j: row(self.ref, base + j)


def back_substitute(held, scratch, top, forward):
    below = scratch.hold(moved(top, 1))
    own = scratch.hold(top)

    def part(index, low, high):
        base = index * BROWS
        value = minus(forward[index], matvec(held, base, 40, left_at, low))
        return minus(value, matvec(held, base, 40, right_at, high))

    one = part(2, below, own)
    one_rows = scratch.hold(one)
    return [part(0, below, one_rows), one, part(1, one_rows, own), top]


def put_cells(ref, cells, copies):
    for c in range(4):
        for d in range(copies):
            for h in range(2):
                ref[d, pl.ds(16 * c + 8 * h, 8), :] = cells[c][h]
            ref[d, pl.ds(64 + c, 1), :] = cells[c][2]
    for d in range(copies):
        ref[d, pl.ds(68, 4), :] = jnp.zeros((4, LANES), FP)


def factor_kernel(
    got_ref, wall_ref, solved_ref, inverse_ref, blocks_ref, held_ref, vectors_ref,
    stage, below, work_blocks, work_diag, low, high, scratch_ref,
):
    groups = lane_ids(1) // COLS
    for g in range(TOTALROWS // 64):
        regs = swap_blocks([got_ref[d, pl.ds(8 * g, 8), :] for d in range(8)])
        for w in range(8):
            stage[pl.ds(64 * g + 8 * w, 8), :] = regs[w]
    for c in range(4):
        for piece in range(5):
            at, step = (RHS_AT + c, 4) if piece == 0 else (COUPLE_AT + 68 * c + piece - 1, 4)
            for h in range(2):
                vectors_ref[pl.ds(VROWS * piece + 16 * c + 8 * h, 8), :] = strided(stage, at + 32 * h, step)
            vectors_ref[pl.ds(VROWS * piece + 64 + c, 1), :] = row(stage, at + 64)
    for piece in range(5):
        vectors_ref[pl.ds(VROWS * piece + 68, 4), :] = jnp.zeros((4, LANES), FP)
    has_below = jnp.where(groups == 0, 0.0, 1.0)
    has_above = jnp.where(groups == GROUPS - 1, 0.0, 1.0)
    for i in range(WIDTH):
        for h in range(2):
            value = strided(stage, 4 * (17 * i + 8 * h) + 3, 4)
            below[pl.ds(17 * i + 8 * h, 8), :] = pltpu.roll(value, COLS, 1) * has_below
    for i in range(0, WIDTH, 8):
        if i < 16:
            value = strided(stage, 4 * (17 * i + 16) + 3, 68)
            below[pl.ds(17 * i + 16, 8, stride=17), :] = pltpu.roll(value, COLS, 1) * has_below
    for at, source in ((288, 4 * 288 + 3), (289, COEF_AT + 3)):
        value = jnp.broadcast_to(row(stage, source), (8, LANES))
        below[pl.ds(at, 1), :] = (pltpu.roll(value, COLS, 1) * has_below)[:1]
    wall = jnp.zeros((1, LANES), FP)
    for kind, level in enumerate(WALLS):
        wall = wall + jnp.where(wall_ref[...] == kind, level, 0.0)
    ids = sub_ids(8)

    def build(c, blocks, blocks_base, diag, diag_base):
        lower, scale, shift = (below, 1, 0) if c == 0 else (stage, 4, c - 1)
        coef_low = row(below, 289) if c == 0 else row(stage, COEF_AT + c - 1)
        coef_up = row(stage, COEF_AT + c)
        on_diag = coef_low + coef_up
        if c == 0:
            on_diag = on_diag + wall * (1.0 - has_below)
        keep = has_above if c == 3 else None

        def up(value):
            return value if keep is None else value * keep

        def at(i, j):
            return 4 * (17 * i + j) + c

        def lower_at(i, j):
            return scale * (17 * i + j) + shift

        for i in range(WIDTH):
            extra = on_diag + row(stage, TIME_AT + 4 * i + c)
            for n in range(4):
                extra = extra + row(stage, COUPLE_AT + 68 * c + 4 * i + n)
            for h in range(2):
                down = -strided(lower, lower_at(8 * h, i), 17 * scale)
                entry = strided(stage, CELL_AT + at(i, 8 * h), 4) - strided(stage, CELL_AT + at(8 * h, i), 68)
                face = strided(stage, at(i, 8 * h), 4)
                if i // 8 == h:
                    here = ids == i % 8
                    entry = entry + jnp.where(here, extra, 0.0)
                    face = face - jnp.where(here, coef_up, 0.0)
                    down = down - jnp.where(here, coef_low, 0.0)
                diag[pl.ds(diag_base + 24 * i + 8 * h, 8), :] = entry
                blocks[pl.ds(blocks_base + 40 * i + 8 * h, 8), :] = down
                blocks[pl.ds(blocks_base + 40 * i + 16 + 8 * h, 8), :] = up(face)
            side = -row(lower, lower_at(16, i))
            face = row(stage, at(i, 16))
            if i < 16:
                corner = row(stage, CELL_AT + at(i, 16)) - row(stage, CELL_AT + at(16, i))
            else:
                corner, side, face = extra, side - coef_low, face - coef_up
            value = row(stage, RIGHT_AT + (16 * c + i if i < 16 else 68 + c))
            packed = jnp.where(ids == 0, side, jnp.where(ids == 1, up(face), jnp.where(ids == 2, value, 0.0)))
            blocks[pl.ds(blocks_base + 40 * i + 32, 8), :] = packed
            diag[pl.ds(diag_base + 24 * i + 16, 8), :] = jnp.where(ids == 0, corner, 0.0)

    B, D = BROWS, DROWS
    build(0, work_blocks, 0, inverse_ref, 0)
    build(2, work_blocks, B, inverse_ref, D)
    build(1, blocks_ref, 0, work_diag, 0)
    build(3, blocks_ref, B, work_diag, D)
    invert_in_place([(inverse_ref, 0), (inverse_ref, D)])
    normalise(inverse_ref, 0, work_blocks, 0, held_ref, 0)
    normalise(inverse_ref, D, work_blocks, B, held_ref, B)

    def turn(source, source_base, result, steps):
        for t in range(BROWS // 8):
            result[pl.ds(8 * t, 8), :] = pltpu.roll(
                tile(source, source_base + 8 * t), (COLS * steps) % LANES, 1
            )

    turn(held_ref, 0, high, -1)
    eliminate(blocks_ref, 0, work_diag, 0, held_ref, 0, held_ref, B, work_blocks, 0, inverse_ref, 2 * D)
    eliminate(blocks_ref, B, work_diag, D, held_ref, B, high, 0, blocks_ref, 2 * B, work_diag, 0)
    invert_in_place([(inverse_ref, 2 * D)])
    normalise(inverse_ref, 2 * D, work_blocks, 0, held_ref, 2 * B)
    turn(held_ref, 2 * B, high, -1)
    eliminate(
        blocks_ref, 2 * B, work_diag, 0, held_ref, 2 * B, high, 0, blocks_ref, 3 * B, inverse_ref, 3 * D
    )
    for k in range(3):
        source = 3 + k
        work_diag[pl.ds(0, D), :] = inverse_ref[pl.ds(source * D, D), :]
        invert_in_place([(inverse_ref, source * D)])
        normalise(inverse_ref, source * D, blocks_ref, source * B, work_blocks, 0)
        turn(work_blocks, 0, low, 2**k)
        turn(work_blocks, 0, high, -(2**k))
        if k < 2:
            new, new_base = blocks_ref, (source + 1) * B
        else:
            new, new_base = work_blocks, B
        eliminate(
            blocks_ref, source * B, work_diag, 0, low, 0, high, 0, new, new_base, inverse_ref, (source + 1) * D
        )
    invert_in_place([(inverse_ref, 6 * D)])
    scratch = Scratch(scratch_ref)
    last = matvec(inverse_ref, 6 * D, 24, plain, lambda j: row(work_blocks, B + 40 * j + 34))
    forward = []
    for index in range(3):
        base = index * B
        forward.append([
            strided(held_ref, base + 34, 40),
            strided(held_ref, base + 320 + 34, 40),
            row(held_ref, base + 640 + 34),
        ])
    put_cells(solved_ref, back_substitute(held_ref, scratch, last, forward), GROUPS)


def solve_kernel(
    all_ref, low_ref, high_ref, index_ref, from_ref, vectors_ref, inverse_ref, blocks_ref, held_ref,
    out_ref, right, scratch_ref,
):
    for t in range(VROWS // 8):
        at = 8 * t
        total = tile(vectors_ref, at)
        for n in range(4):
            lanes = jnp.broadcast_to(index_ref[pl.ds(n, 1), :], (8, LANES))
            source = jnp.broadcast_to(from_ref[pl.ds(n, 1), :], (8, LANES))
            value = jnp.zeros((8, LANES), FP)
            for d in range(GROUPS + 2):
                if d < GROUPS:
                    got = all_ref[d, pl.ds(at, 8), :]
                else:
                    got = tile(low_ref if d == GROUPS else high_ref, at)
                value = jnp.where(source == d, along(got, lanes), value)
            total = total + tile(vectors_ref, VROWS * (n + 1) + at) * value
        right[pl.ds(at, 8), :] = total
    B, D = BROWS, DROWS
    scratch = Scratch(scratch_ref)

    def cell_rows(c):
        return lambda j: row(right, 16 * c + j if j < 16 else 64 + c)

    def cell(c):
        return vector_of(right, 16 * c, 64 + c)

    def apply(index, rows):
        return matvec(inverse_ref, index * D, 24, plain, rows)

    def reduce(value, index, low, high):
        value = minus(value, matvec(blocks_ref, index * B, 40, left_at, low))
        return minus(value, matvec(blocks_ref, index * B, 40, right_at, high))

    zero = apply(0, cell_rows(0))
    two = apply(1, cell_rows(2))
    zero_rows, two_rows = scratch.hold(zero), scratch.hold(two)
    next_zero = scratch.hold(moved(zero, -1))
    one = apply(2, scratch.hold(reduce(cell(1), 0, zero_rows, two_rows)))
    three = reduce(cell(3), 1, two_rows, next_zero)
    one_rows, next_one = scratch.hold(one), scratch.hold(moved(one, -1))
    three = reduce(three, 2, one_rows, next_one)
    for k in range(3):
        scaled = apply(3 + k, scratch.hold(three))
        low, high = scratch.hold(moved(scaled, 2**k)), scratch.hold(moved(scaled, -(2**k)))
        three = reduce(three, 3 + k, low, high)
    last = apply(6, scratch.hold(three))
    cells = back_substitute(held_ref, scratch, last, [zero, two, one])
    for g in range(2):
        regs = []
        for w in range(8):
            v = 8 * g + w
            if v < 8:
                regs.append(cells[v // 2][v % 2])
            elif v == 8:
                ids = sub_ids(8)
                value = jnp.zeros((8, LANES), FP)
                for c in range(4):
                    value = jnp.where(ids == c, cells[c][2], value)
                regs.append(value)
            else:
                regs.append(jnp.zeros((8, LANES), FP))
        regs = swap_blocks(regs)
        for d in range(8):
            out_ref[d, pl.ds(8 * g, 8), :] = regs[d]


def unpack_kernel(got_ref, out_ref):
    flat = out_ref.reshape(4 * WIDTH, LANES)
    for g in range(2):
        regs = swap_blocks([got_ref[d, pl.ds(8 * g, 8), :] for d in range(8)])
        if g == 0:
            for c in range(4):
                for h in range(2):
                    flat[pl.ds(32 * h + c, 8, stride=4), :] = regs[2 * c + h]
        else:
            flat[pl.ds(64, 4), :] = regs[0][:4]


def edge_kernel(top_ref, bottom_ref, top_out_ref, bottom_out_ref):
    top_out_ref[...] = top_ref[0]
    bottom_out_ref[...] = bottom_ref[0]


def shape(*dims):
    return jax.ShapeDtypeStruct(dims, FP)


def call(kernel, outputs, scratch, args, flops, name, limit=16, **more):
    return pl.pallas_call(
        kernel,
        out_shape=outputs,
        scratch_shapes=[pltpu.VMEM(dims, FP) if isinstance(dims, tuple) else dims for dims in scratch],
        compiler_params=pltpu.CompilerParams(vmem_limit_bytes=limit * 2**20),
        cost_estimate=pl.CostEstimate(flops=flops, bytes_accessed=1000000, transcendentals=0),
        name=name,
        **more,
    )(*args)


def across(value):
    return lax.all_to_all(value, "line", 0, 0, tiled=True)


def on_device(
    face_coef, face_mix, cell_mix, time_term, couple, rhs, start_delta, neighbours, wall_type
):
    count = lax.axis_size("surf")
    up = [(i, (i + 1) % count) for i in range(count)]
    down = [(target, source) for source, target in up]
    lines = wall_type.shape[0]
    place = lax.axis_index("line")
    start = start_delta.transpose(1, 0, 2)
    rhs_rows = rhs.transpose(1, 0, 2)
    couple_rows = couple.transpose(0, 2, 1, 3).reshape(4 * WIDTH, 4, lines)
    face, cell = [a.transpose(1, 2, 0, 3).reshape(WIDTH * WIDTH, 4, lines) for a in (face_mix, cell_mix)]
    low = lax.ppermute(start, "surf", up)
    high = lax.ppermute(start, "surf", down)

    surf_place = lax.axis_index("surf")
    local = (neighbours - (surf_place * lines - COLS)) % (lines * count)
    is_low = local < COLS
    is_own = (local >= COLS) & (local < COLS + lines)
    valid = neighbours >= 0
    own_index = jnp.clip(local - COLS, 0, lines - 1)
    kind = jnp.where(is_own, 0, jnp.where(is_low, 1, 2))
    kind = jnp.where(valid, kind, -1)
    index = jnp.where(is_own, own_index, jnp.where(is_low, local + lines - COLS, local - lines - COLS))
    index = jnp.clip(index, 0, lines - 1)
    source = jnp.where(is_own, own_index // COLS, jnp.where(is_low, GROUPS, GROUPS + 1))
    source = jnp.where(valid, source, -1)
    offset = index % COLS

    def for_group(array):
        mine = lax.dynamic_slice_in_dim(array, place * COLS, COLS, axis=array.ndim - 1)
        return jnp.tile(mine, (1, GROUPS))

    group_offset = for_group(offset) + (jnp.arange(lines, dtype=jnp.int32) // COLS * COLS)[None]
    group_source = for_group(source)
    group_wall = for_group(wall_type[None])

    packed = call(
        pack_kernel,
        shape(GROUPS, TOTALROWS // 8, LANES),
        [(40, LANES)],
        (face_coef, face, cell, time_term.transpose(1, 0, 2), couple_rows, rhs_rows),
        20000000,
        "pack",
    )
    any_place = pl.BlockSpec(memory_space=pl.ANY)
    packed = call(
        right_kernel,
        shape(GROUPS, TOTALROWS // 8, LANES),
        [(GROUPS, 16, LANES), pltpu.SemaphoreType.DMA(())],
        (start, low, high, index, kind, couple_rows, rhs_rows, packed),
        1000000,
        "right",
        in_specs=[pl.BlockSpec(memory_space=pltpu.VMEM)] * 7 + [any_place],
        out_specs=any_place,
        input_output_aliases={7: 0},
    )
    packed, group_offset, group_source, group_wall = lax.optimization_barrier(
        (packed, group_offset, group_source, group_wall)
    )
    received = across(packed)
    solved, inverses, blocks, held, vectors = call(
        factor_kernel,
        (
            shape(GROUPS, VROWS, LANES),
            shape(7 * DROWS, LANES),
            shape(6 * BROWS, LANES),
            shape(3 * BROWS, LANES),
            shape(5 * VROWS, LANES),
        ),
        [
            (TOTALROWS, LANES), (BELOWROWS, LANES), (2 * BROWS, LANES), (2 * DROWS, LANES),
            (BROWS, LANES), (BROWS, LANES), (24 * 4, LANES),
        ],
        (received, group_wall),
        30000000,
        "factor",
    )
    everyone = across(solved)
    top, bottom = call(
        edge_kernel, (shape(VROWS, LANES), shape(VROWS, LANES)), [], (everyone, everyone), 1000, "edge", 1,
        grid=(1,),
        in_specs=[pl.BlockSpec((1, VROWS, LANES), lambda i: (GROUPS - 1, 0, 0)), pl.BlockSpec((1, VROWS, LANES), lambda i: (0, 0, 0))],
    )
    low = lax.ppermute(top, "surf", up)
    high = lax.ppermute(bottom, "surf", down)
    sent = call(
        solve_kernel,
        shape(GROUPS, 16, LANES),
        [(VROWS, LANES), (24 * 24, LANES)],
        (everyone, low, high, group_offset, group_source, vectors, inverses, blocks, held),
        3000000,
        "solve",
    )
    done = call(unpack_kernel, shape(WIDTH, 4, LANES), [], (across(sent),), 100000, "unpack")
    return done.transpose(1, 0, 2)


def solution(mesh):
    placed = (
        P("line", "surf"),
        P("line", None, None, "surf"),
        P("line", None, None, "surf"),
        P("line", None, "surf"),
        P("line", None, None, "surf"),
        P("line", None, "surf"),
        P("line", None, "surf"),
        P(None, "surf"),
        P("surf"),
    )
    return jax.shard_map(
        on_device, mesh=mesh, in_specs=placed, out_specs=P("line", None, "surf"), check_vma=False
    )
```

time: 390 us -> 97.4 us (0.25); the launches traced: 385 us -> 96.8 us
  other arithmetic: 181 us -> 0.73 us
  waiting for transfers between devices: 78.7 us -> 5.49 us
  local copies, waits for them, and re-layouts: 68.2 us -> 6.32 us
  blocking collectives: 0 us -> 46.3 us
  Pallas kernels: 0 us -> 29.3 us
  starting transfers between devices: 33.3 us -> 8.56 us
  between operations: 14.1 us -> 0.08 us
  loops' own time: 9.01 us -> 0 us
    reduce_sum x103 -> x0, other arithmetic: 63.4 us -> none  [the longest x70 47.1 us: matrix_vector(): return jnp.sum(matrix_left * vector_right[None, :, :], axis=1)]
    all_to_all x0 -> x3, blocking collectives: none -> 46.3 us  [across(): return lax.all_to_all(value, 'line', 0, 0, tiled=True)]
    all_gather x1 -> x0, waiting for transfers between devices: 37.8 us -> none  [in_one_piece(): lax.all_gather(both, axis, axis=dim, tiled=True)]
    select_n x198 -> x2, other arithmetic: 33.3 us -> 0.72 us  [the longest x1 0.7 us: on_device(): source = jnp.where(valid, source, -1)]
    dynamic_update_slice x36 -> x0, other arithmetic: 32.4 us -> none  [the longest x8 12.6 us: on_device(): lax.scan(chain_factor, zero_matrix, (all_lower, all_diag, all_upper))]
    pallas_call x0 -> x6, Pallas kernels: none -> 29.3 us  [call(): pl.pallas_call(kernel, out_shape=outputs, scratch_shapes=[pltpu.VMEM(dims...]
    ppermute x10 -> x4, waiting for transfers between devices: 27.6 us -> 5.49 us  [the longest x1 4.43 us: on_device(): high = lax.ppermute(bottom, 'surf', down)]
    sub x41 -> x0, other arithmetic: 21.7 us -> none  [the longest x22 14.5 us: vector_back(): solved_now = forward_value - matrix_vector(coupler, solved_above)]
  transfers between devices with their start and end apart: 13 -> 4, of which waited for: 11 -> 2; matrix products, arithmetic and copies ran while one was open for 5% -> 2% of each run, Pallas kernels for 0% -> 6%
where the time goes in v1:
time: 97.4 us; the launch traced here: 96.8 us
  blocking collectives  46.3 us (48%)
  Pallas kernels  29.3 us (30%)
  starting transfers between devices  8.56 us (9%)
  local copies, waits for them, and re-layouts  6.32 us (6%)
  waiting for transfers between devices  5.49 us (6%)
    all_to_all x3, blocking collectives, across(): return lax.all_to_all(value, 'line', 0, 0, tiled=True)  46.3 us
    pallas_call x6, Pallas kernels, call(): pl.pallas_call(kernel, out_shape=outputs, scratch_shapes=[pltpu.VMEM(dims...  29.3 us
    unnamed x14, local copies, waits for them, and re-layouts  5.25 us
    ppermute x1, starting transfers between devices, on_device(): low = lax.ppermute(top, 'surf', up)  4.7 us
    ppermute x1, waiting for transfers between devices, on_device(): high = lax.ppermute(bottom, 'surf', down)  4.43 us
    ppermute x1, starting transfers between devices, on_device(): low = lax.ppermute(start, 'surf', up)  3.18 us
  transfers between devices with their start and end apart: 4, of which 2 were waited for; matrix products, arithmetic and copies ran while one was open for 2% of the time, Pallas kernels for 6%

profile of v1, /device:TPU:99, one launch (start us, length us, event | category | flops | bytes accessed | tf_op | source)
XLA Modules:
  0.0 96.8 jit_solution(10524555985191723242)
XLA Ops:
  0.0 0.7 collective-permute-start.1
  0.7 3.2 %collective-permute-start = (f32[17,4,128]{2,1,0:T(4,128)}, f32[17,4,128]{2,1,0:T(4,128)S(1)}, u32[]{:S(2)}, u32[]{:S(2)}) collective-permute-start(f32[17,4,128]{2,1,0:T(4,128)} %bitcast.21), channel_id=1, source_target_pairs={{0,1},{1,2},{2,3},{3,4},{4,5},{5,6},{6,7},{7,8},{8,9},{9,10},{10,1... | collective-permute-start | bytes 104456 | tf_op jit(solution)/shard_map/ppermute | solution.py:529
  3.9 0.7 fusion.4
  4.6 0.1 constant_dynamic-slice_fusion
  4.7 0.0 copy-start.5
  4.7 0.1 tile.13
  4.8 0.7 dynamic-slice.3
  5.5 0.1 tile.32.wall_ref
  5.6 0.1 tile.30.from_ref
  5.7 0.0 copy-start
  5.7 1.1 %copy-done = f32[4,17,17,128]{3,0,2,1:T(4,128)S(1)} copy-done((f32[4,17,17,128]{3,0,2,1:T(4,128)S(1)}, f32[4,17,17,128]{3,0,2,1:T(4,128)}, u32[]{:S(2)}) %copy-start) | copy-done | bytes 591896
  6.7 0.0 copy-start.1
  6.7 1.1 %copy-done.1 = f32[4,17,17,128]{3,0,2,1:T(4,128)S(1)} copy-done((f32[4,17,17,128]{3,0,2,1:T(4,128)S(1)}, f32[4,17,17,128]{3,0,2,1:T(4,128)}, u32[]{:S(2)}) %copy-start.1) | copy-done | bytes 591896
  7.8 0.9 copy-done.2
  8.7 0.8 copy-done.3
  9.5 0.8 copy-done.4
  10.2 0.7 copy-done.6
  10.9 5.6 %pack.1._ = f32[8,360,128]{2,1,0:T(8,128)S(1)} custom-call(f32[4,128]{1,0:T(4,128)S(1)} %copy-done.6, f32[289,4,128]{2,1,0:T(4,128)S(1)} %bitcast.13, f32[289,4,128]{2,1,0:T(4,128)S(1)} %bitcast.14, f32[17,4,128]{2,1,0:T(4,128)S(1)} %bitcast.19, f32[68,4,128]{2,1,0:T(4,128)S(1)} %bitcast.15, f32[17,4,128]{2,1,0:T(4,128)S(1)} %bitcast.17), custom_call_target="tpu_custom_call" | custom-call | flops 20000000 | bytes 1000000 | tf_op jit(solution)/shard_map/pack/pallas_call | solution.py:502
  16.5 0.0 collective-permute-done.1.high_ref
  16.5 0.0 collective-permute-done.low_ref
  16.5 0.0 copy-done.5
  16.5 0.5 right.1
  17.1 25.7 %all_to_all.15.got_ref = f32[8,360,128]{2,1,0:T(8,128)S(1)} all-to-all(f32[8,360,128]{2,1,0:T(8,128)S(1)} %right.1), channel_id=1, replica_groups=mesh['line'=8,'surf'=32] {'line'}, dimensions={0} | all-to-all | bytes 2949120 | tf_op jit(solution)/shard_map/all_to_all | solution.py:514
  42.8 20.5 %factor.1 = (f32[8,72,128]{2,1,0:T(8,128)S(1)}, f32[2856,128]{1,0:T(8,128)S(1)}, f32[4080,128]{1,0:T(8,128)S(1)}, f32[2040,128]{1,0:T(8,128)S(1)}, f32[360,128]{1,0:T(8,128)S(1)}) custom-call(f32[8,360,128]{2,1,0:T(8,128)S(1)} %all_to_all.15.got_ref, s32[1,128]{1,0:T(1,128)S(1)} %tile.32.wall_ref), custom_call_target="tpu_custom_call" | custom-call | flops 30000000 | bytes 1000000 | tf_op jit(solution)/shard_map/factor/pallas_call | solution.py:502
  63.3 11.5 %all_to_all.16.top_ref.bottom_ref.all_ref = f32[8,72,128]{2,1,0:T(8,128)S(1)} all-to-all(f32[8,72,128]{2,1,0:T(8,128)S(1)} %get-tuple-element.18), channel_id=1, replica_groups=mesh['line'=8,'surf'=32] {'line'}, dimensions={0} | all-to-all | bytes 589824 | tf_op jit(solution)/shard_map/all_to_all | solution.py:514
  74.8 4.7 %collective-permute-start.2 = (f32[72,128]{1,0:T(8,128)S(1)}, f32[72,128]{1,0:T(8,128)S(1)}, u32[]{:S(2)}, u32[]{:S(2)}) collective-permute-start(f32[72,128]{1,0:T(8,128)S(1)} %get-tuple-element.19), channel_id=1, source_target_pairs={{0,1},{1,2},{2,3},{3,4},{4,5},{5,6},{6,7},{7,8},{8,9},{9,10},{10,1... | collective-permute-start | bytes 110600 | tf_op jit(solution)/shard_map/ppermute | solution.py:601
  79.5 0.0 collective-permute-start.3
  79.5 1.1 %collective-permute-done.2.low_ref = f32[72,128]{1,0:T(8,128)S(1)} collective-permute-done((f32[72,128]{1,0:T(8,128)S(1)}, f32[72,128]{1,0:T(8,128)S(1)}, u32[]{:S(2)}, u32[]{:S(2)}) %collective-permute-start.2) | collective-permute-done | bytes 36896 | tf_op jit(solution)/shard_map/ppermute | solution.py:601
  80.6 4.4 %collective-permute-done.3.high_ref = f32[72,128]{1,0:T(8,128)S(1)} collective-permute-done((f32[72,128]{1,0:T(8,128)S(1)}, f32[72,128]{1,0:T(8,128)S(1)}, u32[]{:S(2)}, u32[]{:S(2)}) %collective-permute-start.3) | collective-permute-done | bytes 36896 | tf_op jit(solution)/shard_map/ppermute | solution.py:602
  85.0 1.9 %solve.1 = f32[8,16,128]{2,1,0:T(8,128)S(1)} custom-call(f32[8,72,128]{2,1,0:T(8,128)S(1)} %all_to_all.16.top_ref.bottom_ref.all_ref, f32[72,128]{1,0:T(8,128)S(1)} %collective-permute-done.2.low_ref, f32[72,128]{1,0:T(8,128)S(1)} %collective-permute-done.3.high_ref, s32[4,128]{1,0:T(4,128)S(1)} %broadcast_add_fusion.index_ref, s32[4,128]{1,0:T(4,128)S(1)} %tile.30.from_ref, ...), custom_call_target="tpu_custom_call" | custom-call | flops 3000000 | bytes 1000000 | tf_op jit(solution)/shard_map/solve/pallas_call | solution.py:502
  86.9 9.1 %all_to_all.17.got_ref = f32[8,16,128]{2,1,0:T(8,128)S(1)} all-to-all(f32[8,16,128]{2,1,0:T(8,128)S(1)} %solve.1), channel_id=1, replica_groups=mesh['line'=8,'surf'=32] {'line'}, dimensions={0} | all-to-all | bytes 131072 | tf_op jit(solution)/shard_map/all_to_all | solution.py:514
  96.0 0.8 unpack.1
  (11 shorter events, 0.1 us)
Async XLA Ops:
  0.0 16.5 %collective-permute-start.1 = (f32[17,4,128]{2,1,0:T(4,128)}, f32[17,4,128]{2,1,0:T(4,128)S(1)}, u32[]{:S(2)}, u32[]{:S(2)}) collective-permute-start(f32[17,4,128]{2,1,0:T(4,128)} %bitcast.20), channel_id=1, source_target_pairs={{1,0},{2,1},{3,2},{4,3},{5,4},{6,5},{7,6},{8,7},{9,8},{10,9},{11,1... | collective-permute-start | bytes 104456 | tf_op jit(solution)/shard_map/ppermute | solution.py:530
  0.7 15.8 %collective-permute-start = (f32[17,4,128]{2,1,0:T(4,128)}, f32[17,4,128]{2,1,0:T(4,128)S(1)}, u32[]{:S(2)}, u32[]{:S(2)}) collective-permute-start(f32[17,4,128]{2,1,0:T(4,128)} %bitcast.21), channel_id=1, source_target_pairs={{0,1},{1,2},{2,3},{3,4},{4,5},{5,6},{6,7},{7,8},{8,9},{9,10},{10,1... | collective-permute-start | bytes 104456 | tf_op jit(solution)/shard_map/ppermute | solution.py:529
  4.7 11.9 %copy-start.5 = (f32[4,17,128]{2,0,1:T(4,128)S(1)}, f32[4,17,128]{2,0,1:T(4,128)}, u32[]{:S(2)}) copy-start(f32[4,17,128]{2,0,1:T(4,128)} %param.15) | copy-start | bytes 104452
  5.7 1.1 %copy-start = (f32[4,17,17,128]{3,0,2,1:T(4,128)S(1)}, f32[4,17,17,128]{3,0,2,1:T(4,128)}, u32[]{:S(2)}) copy-start(f32[4,17,17,128]{3,0,2,1:T(4,128)} %param.10) | copy-start | bytes 1775620
  6.7 1.1 %copy-start.1 = (f32[4,17,17,128]{3,0,2,1:T(4,128)S(1)}, f32[4,17,17,128]{3,0,2,1:T(4,128)}, u32[]{:S(2)}) copy-start(f32[4,17,17,128]{3,0,2,1:T(4,128)} %param.11) | copy-start | bytes 1775620
  7.8 0.9 copy-start.2
  8.7 0.8 copy-start.3
  9.5 0.8 copy-start.4
  10.2 0.7 copy-start.6
  74.8 5.8 %collective-permute-start.2 = (f32[72,128]{1,0:T(8,128)S(1)}, f32[72,128]{1,0:T(8,128)S(1)}, u32[]{:S(2)}, u32[]{:S(2)}) collective-permute-start(f32[72,128]{1,0:T(8,128)S(1)} %get-tuple-element.19), channel_id=1, source_target_pairs={{0,1},{1,2},{2,3},{3,4},{4,5},{5,6},{6,7},{7,8},{8,9},{9,10},{10,1... | collective-permute-start | bytes 110600 | tf_op jit(solution)/shard_map/ppermute | solution.py:601
  79.5 5.5 %collective-permute-start.3 = (f32[72,128]{1,0:T(8,128)S(1)}, f32[72,128]{1,0:T(8,128)S(1)}, u32[]{:S(2)}, u32[]{:S(2)}) collective-permute-start(f32[72,128]{1,0:T(8,128)S(1)} %get-tuple-element.20), channel_id=1, source_target_pairs={{1,0},{2,1},{3,2},{4,3},{5,4},{6,5},{7,6},{8,7},{9,8},{10,9},{11,1... | collective-permute-start | bytes 110600 | tf_op jit(solution)/shard_map/ppermute | solution.py:602

commit v2 on v1

--- a/solution.py
+++ b/solution.py
@@ -13,9 +13,14 @@
 BROWS = 40 * WIDTH
 BELOWROWS = 296
 VROWS = 72
-MATRIX_GROUPS = 43
-TOTALROWS = 64 * (MATRIX_GROUPS + 2)
-CELL_AT, TIME_AT, RHS_AT, COUPLE_AT, COEF_AT, RIGHT_AT = 1160, 2320, 2392, 2464, 2736, 2752
+MATRIX_BLOCKS = 17
+TOTALROWS = 128 * (MATRIX_BLOCKS + 1)
+SKEW_TILES = WIDTH * (WIDTH - 1) // 2
+SKEW_AT = 1160
+TIME_AT = SKEW_AT + 4 * SKEW_TILES
+RHS_AT, COUPLE_AT = TIME_AT + 72, TIME_AT + 144
+COEF_AT = COUPLE_AT + 272
+RIGHT_AT = 128 * MATRIX_BLOCKS
 WALLS = (0.5, 4.0, 32.0)
 FP = jnp.float32
 
@@ -28,19 +33,18 @@
     return lax.broadcasted_iota(jnp.int32, (rows, LANES), 0)
 
 
-def swap_blocks(regs):
-    lanes = lane_ids(8)
-    for k in (1, 2, 4):
-        high = (lanes // (COLS * k)) % 2 == 1
-        result = list(regs)
-        for a in range(8):
-            if a & k:
-                continue
-            b = a | k
-            result[a] = jnp.where(high, pltpu.roll(regs[b], COLS * k, 1), regs[a])
-            result[b] = jnp.where(high, regs[b], pltpu.roll(regs[a], LANES - COLS * k, 1))
-        regs = result
-    return regs
+def skew_tile(i, j):
+    return 16 * i - i * (i - 1) // 2 + j - i - 1
+
+
+def split_lines(tiles, out_ref, at):
+    turned = jnp.concatenate(tiles, axis=0).T
+    for d in range(GROUPS):
+        out_ref[d, pl.ds(at, COLS), :] = turned[COLS * d : COLS * (d + 1)]
+
+
+def join_lines(got_ref, at):
+    return jnp.concatenate([got_ref[d, pl.ds(at, COLS), :] for d in range(GROUPS)], axis=0).T
 
 
 def row(ref, at):
@@ -52,7 +56,7 @@
 
 
 def strided(ref, at, stride):
-    return ref[pl.ds(at, 8, stride=stride), :]
+    return ref[pl.ds(at, 8, stride=stride), :] if stride > 1 else tile(ref, at)
 
 
 def along(value, lanes):
@@ -61,27 +65,39 @@
     return jnp.take_along_axis(value, lanes, axis=1, mode="promise_in_bounds")[:rows]
 
 
-def pack_kernel(coef_ref, face_ref, cell_ref, time_ref, couple_ref, rhs_ref, out_ref, stage):
+def pack_kernel(
+    coef_in, face_in, cell_in, time_in, couple_in, rhs_in, out_ref, couple_ref, rhs_ref,
+    coef_ref, face_ref, cell_ref, time_ref, skew_ref, stage, sems,
+):
+    pairs = (
+        (cell_in, cell_ref), (face_in, face_ref), (time_in, time_ref), (couple_in, couple_ref),
+        (rhs_in, rhs_ref), (coef_in, coef_ref),
+    )
+    copies = [pltpu.make_async_copy(a, b, sems.at[n]) for n, (a, b) in enumerate(pairs)]
+    for copy in copies:
+        copy.start()
+    copies[0].wait()
+    for i in range(WIDTH):
+        for j in range(i + 1, WIDTH):
+            skew_ref[skew_tile(i, j)] = cell_ref[WIDTH * i + j] - cell_ref[WIDTH * j + i]
+    for copy in copies[1:]:
+        copy.wait()
     pieces = []
-    for ref in (face_ref, cell_ref, time_ref, rhs_ref, couple_ref, coef_ref):
+    tails = 0
+    for ref in (face_ref, skew_ref, time_ref, rhs_ref, couple_ref, coef_ref):
         rows = ref.size // LANES
         flat = ref if len(ref.shape) == 2 else ref.reshape(rows, LANES)
         for at in range(0, rows - 7, 8):
             pieces.append((flat, at))
         if rows % 8:
-            spot = 8 * len([p for p in pieces if p[0] is stage])
-            stage[pl.ds(spot, 8), :] = jnp.zeros((8, LANES), FP)
-            stage[pl.ds(spot, rows % 8), :] = flat[pl.ds(rows - rows % 8, rows % 8), :]
-            pieces.append((stage, spot))
+            stage[pl.ds(8 * tails, 8), :] = jnp.zeros((8, LANES), FP)
+            stage[pl.ds(8 * tails, rows % 8), :] = flat[pl.ds(rows - rows % 8, rows % 8), :]
+            pieces.append((stage, 8 * tails))
+            tails += 1
     zeros = jnp.zeros((8, LANES), FP)
-    for g in range(MATRIX_GROUPS):
-        regs = []
-        for w in range(8):
-            n = 8 * g + w
-            regs.append(tile(*pieces[n]) if n < len(pieces) else zeros)
-        regs = swap_blocks(regs)
-        for d in range(8):
-            out_ref[d, pl.ds(8 * g, 8), :] = regs[d]
+    for g in range(MATRIX_BLOCKS):
+        part = pieces[16 * g : 16 * g + 16]
+        split_lines([tile(*p) for p in part] + [zeros] * (16 - len(part)), out_ref, COLS * g)
 
 
 def right_kernel(
@@ -118,12 +134,8 @@
         return value
 
     regs.append(total(lambda ref: tile(ref, 60), last_weight))
-    zeros = jnp.zeros((8, LANES), FP)
-    for g in range(2):
-        part = swap_blocks((regs + [zeros] * 7)[8 * g : 8 * g + 8])
-        for d in range(8):
-            stage[d, pl.ds(8 * g, 8), :] = part[d]
-    copy = pltpu.make_async_copy(stage, out_ref.at[:, pl.ds(8 * MATRIX_GROUPS, 16), :], sem)
+    split_lines(regs + [jnp.zeros((8, LANES), FP)] * 7, stage, 0)
+    copy = pltpu.make_async_copy(stage, out_ref.at[:, pl.ds(COLS * MATRIX_BLOCKS, COLS), :], sem)
     copy.start()
     copy.wait()
 
@@ -157,54 +169,69 @@
                 ref[pl.ds(base + 24 * k + 8 * v, 8), :] = scaled[v]
 
 
+def by_rows(step):
+    lax.fori_loop(0, WIDTH // 2, lambda t, _: step([2 * t, 2 * t + 1]), 0)
+    step([WIDTH - 1])
+
+
+def plus(total, term):
+    return term if total is None else total + term
+
+
 def normalise(inverse, inverse_base, source, source_base, result, result_base):
-    def step(i, _):
-        at = pl.multiple_of(24 * i, 8)
-        sums = [None] * 5
+    def step(rows):
+        starts = [pl.multiple_of(24 * i, 8) for i in rows]
+        sums = [[None] * 5 for _ in rows]
         for j in range(WIDTH):
-            factor = row(inverse, inverse_base + at + j)
+            factors = [row(inverse, inverse_base + at + j) for at in starts]
             for v in range(5):
-                term = factor * tile(source, source_base + 40 * j + 8 * v)
-                sums[v] = term if j == 0 else sums[v] + term
-        to = pl.multiple_of(40 * i, 8)
-        for v in range(5):
-            result[pl.ds(result_base + to + 8 * v, 8), :] = sums[v]
+                value = tile(source, source_base + 40 * j + 8 * v)
+                for r, factor in enumerate(factors):
+                    sums[r][v] = plus(sums[r][v], factor * value)
+        for r, i in enumerate(rows):
+            to = pl.multiple_of(40 * i, 8)
+            for v in range(5):
+                result[pl.ds(result_base + to + 8 * v, 8), :] = sums[r][v]
         return 0
 
-    lax.fori_loop(0, WIDTH, step, 0)
+    by_rows(step)
 
 
 def eliminate(blocks, base, diag, diag_base, low, low_base, high, high_base, new, new_base, new_diag, new_diag_base):
     ids = sub_ids(8)
 
-    def step(i, _):
-        at = pl.multiple_of(40 * i, 8)
-        first, second = [None] * 5, [None] * 5
+    def step(rows):
+        starts = [pl.multiple_of(40 * i, 8) for i in rows]
+        firsts = [[None] * 5 for _ in rows]
+        seconds = [[None] * 5 for _ in rows]
         for j in range(WIDTH):
-            below = row(blocks, base + at + left_at(j))
-            above = row(blocks, base + at + right_at(j))
+            below = [row(blocks, base + at + left_at(j)) for at in starts]
+            above = [row(blocks, base + at + right_at(j)) for at in starts]
             for v in range(5):
-                term = below * tile(low, low_base + 40 * j + 8 * v)
-                first[v] = term if j == 0 else first[v] + term
-                term = above * tile(high, high_base + 40 * j + 8 * v)
-                second[v] = term if j == 0 else second[v] + term
-        for v in range(2):
-            new[pl.ds(new_base + at + 8 * v, 8), :] = -first[v]
-            new[pl.ds(new_base + at + 16 + 8 * v, 8), :] = -second[2 + v]
-        rest = tile(blocks, base + at + 32) - first[4] - second[4]
-        rest = jnp.where(ids == 0, -first[4], jnp.where(ids == 1, -second[4], rest))
-        new[pl.ds(new_base + at + 32, 8), :] = rest
-        to = pl.multiple_of(24 * i, 8)
-        for v in range(2):
-            new_diag[pl.ds(new_diag_base + to + 8 * v, 8), :] = (
-                tile(diag, diag_base + to + 8 * v) - first[2 + v] - second[v]
+                value = tile(low, low_base + 40 * j + 8 * v)
+                for r, factor in enumerate(below):
+                    firsts[r][v] = plus(firsts[r][v], factor * value)
+                value = tile(high, high_base + 40 * j + 8 * v)
+                for r, factor in enumerate(above):
+                    seconds[r][v] = plus(seconds[r][v], factor * value)
+        for at, i, first, second in zip(starts, rows, firsts, seconds):
+            for v in range(2):
+                new[pl.ds(new_base + at + 8 * v, 8), :] = -first[v]
+                new[pl.ds(new_base + at + 16 + 8 * v, 8), :] = -second[2 + v]
+            rest = tile(blocks, base + at + 32) - first[4] - second[4]
+            rest = jnp.where(ids == 0, -first[4], jnp.where(ids == 1, -second[4], rest))
+            new[pl.ds(new_base + at + 32, 8), :] = rest
+            to = pl.multiple_of(24 * i, 8)
+            for v in range(2):
+                new_diag[pl.ds(new_diag_base + to + 8 * v, 8), :] = (
+                    tile(diag, diag_base + to + 8 * v) - first[2 + v] - second[v]
+                )
+            new_diag[pl.ds(new_diag_base + to + 16, 8), :] = (
+                tile(diag, diag_base + to + 16) - pltpu.roll(first[4], 7, 0) - second[4]
             )
-        new_diag[pl.ds(new_diag_base + to + 16, 8), :] = (
-            tile(diag, diag_base + to + 16) - pltpu.roll(first[4], 7, 0) - second[4]
-        )
         return 0
 
-    lax.fori_loop(0, WIDTH, step, 0)
+    by_rows(step)
 
 
 def matvec(ref, base, stride, at, value_row):
@@ -279,13 +306,22 @@
 
 def factor_kernel(
     got_ref, wall_ref, solved_ref, inverse_ref, blocks_ref, held_ref, vectors_ref,
-    stage, below, work_blocks, work_diag, low, high, scratch_ref,
+    stage_tiles, turned_tiles, skew_tiles, below, work_blocks, work_diag, low, high, scratch_ref,
 ):
+    stage = stage_tiles.reshape(TOTALROWS, LANES)
+    turned = turned_tiles.reshape(4 * WIDTH * WIDTH, LANES)
+    skew = skew_tiles.reshape(4 * WIDTH * WIDTH, LANES)
     groups = lane_ids(1) // COLS
-    for g in range(TOTALROWS // 64):
-        regs = swap_blocks([got_ref[d, pl.ds(8 * g, 8), :] for d in range(8)])
-        for w in range(8):
-            stage[pl.ds(64 * g + 8 * w, 8), :] = regs[w]
+    for g in range(MATRIX_BLOCKS + 1):
+        stage[pl.ds(128 * g, 128), :] = join_lines(got_ref, COLS * g)
+    for i in range(WIDTH):
+        skew_tiles[WIDTH * i + i] = jnp.zeros((4, LANES), FP)
+        for j in range(WIDTH):
+            turned_tiles[WIDTH * i + j] = stage_tiles[WIDTH * j + i]
+            if j > i:
+                value = stage_tiles[SKEW_AT // 4 + skew_tile(i, j)]
+                skew_tiles[WIDTH * i + j] = value
+                skew_tiles[WIDTH * j + i] = -value
     for c in range(4):
         for piece in range(5):
             at, step = (RHS_AT + c, 4) if piece == 0 else (COUPLE_AT + 68 * c + piece - 1, 4)
@@ -298,11 +334,11 @@
     has_above = jnp.where(groups == GROUPS - 1, 0.0, 1.0)
     for i in range(WIDTH):
         for h in range(2):
-            value = strided(stage, 4 * (17 * i + 8 * h) + 3, 4)
+            value = strided(turned, 4 * (17 * i + 8 * h) + 3, 4)
             below[pl.ds(17 * i + 8 * h, 8), :] = pltpu.roll(value, COLS, 1) * has_below
     for i in range(0, WIDTH, 8):
         if i < 16:
-            value = strided(stage, 4 * (17 * i + 16) + 3, 68)
+            value = strided(turned, 4 * (17 * i + 16) + 3, 68)
             below[pl.ds(17 * i + 16, 8, stride=17), :] = pltpu.roll(value, COLS, 1) * has_below
     for at, source in ((288, 4 * 288 + 3), (289, COEF_AT + 3)):
         value = jnp.broadcast_to(row(stage, source), (8, LANES))
@@ -313,7 +349,7 @@
     ids = sub_ids(8)
 
     def build(c, blocks, blocks_base, diag, diag_base):
-        lower, scale, shift = (below, 1, 0) if c == 0 else (stage, 4, c - 1)
+        lower, scale, shift = (below, 1, 0) if c == 0 else (turned, 4, c - 1)
         coef_low = row(below, 289) if c == 0 else row(stage, COEF_AT + c - 1)
         coef_up = row(stage, COEF_AT + c)
         on_diag = coef_low + coef_up
@@ -335,8 +371,8 @@
             for n in range(4):
                 extra = extra + row(stage, COUPLE_AT + 68 * c + 4 * i + n)
             for h in range(2):
-                down = -strided(lower, lower_at(8 * h, i), 17 * scale)
-                entry = strided(stage, CELL_AT + at(i, 8 * h), 4) - strided(stage, CELL_AT + at(8 * h, i), 68)
+                down = -strided(lower, lower_at(i, 8 * h), scale)
+                entry = strided(skew, at(i, 8 * h), 4)
                 face = strided(stage, at(i, 8 * h), 4)
                 if i // 8 == h:
                     here = ids == i % 8
@@ -346,10 +382,10 @@
                 diag[pl.ds(diag_base + 24 * i + 8 * h, 8), :] = entry
                 blocks[pl.ds(blocks_base + 40 * i + 8 * h, 8), :] = down
                 blocks[pl.ds(blocks_base + 40 * i + 16 + 8 * h, 8), :] = up(face)
-            side = -row(lower, lower_at(16, i))
+            side = -row(lower, lower_at(i, 16))
             face = row(stage, at(i, 16))
             if i < 16:
-                corner = row(stage, CELL_AT + at(i, 16)) - row(stage, CELL_AT + at(16, i))
+                corner = row(skew, at(i, 16))
             else:
                 corner, side, face = extra, side - coef_low, face - coef_up
             value = row(stage, RIGHT_AT + (16 * c + i if i < 16 else 68 + c))
@@ -458,35 +494,22 @@
         three = reduce(three, 3 + k, low, high)
     last = apply(6, scratch.hold(three))
     cells = back_substitute(held_ref, scratch, last, [zero, two, one])
-    for g in range(2):
-        regs = []
-        for w in range(8):
-            v = 8 * g + w
-            if v < 8:
-                regs.append(cells[v // 2][v % 2])
-            elif v == 8:
-                ids = sub_ids(8)
-                value = jnp.zeros((8, LANES), FP)
-                for c in range(4):
-                    value = jnp.where(ids == c, cells[c][2], value)
-                regs.append(value)
-            else:
-                regs.append(jnp.zeros((8, LANES), FP))
-        regs = swap_blocks(regs)
-        for d in range(8):
-            out_ref[d, pl.ds(8 * g, 8), :] = regs[d]
+    regs = [cells[c][h] for c in range(4) for h in range(2)]
+    value = jnp.zeros((8, LANES), FP)
+    for c in range(4):
+        value = jnp.where(sub_ids(8) == c, cells[c][2], value)
+    regs.append(value)
+    split_lines(regs + [jnp.zeros((8, LANES), FP)] * 7, out_ref, 0)
 
 
 def unpack_kernel(got_ref, out_ref):
     flat = out_ref.reshape(4 * WIDTH, LANES)
-    for g in range(2):
-        regs = swap_blocks([got_ref[d, pl.ds(8 * g, 8), :] for d in range(8)])
-        if g == 0:
-            for c in range(4):
-                for h in range(2):
-                    flat[pl.ds(32 * h + c, 8, stride=4), :] = regs[2 * c + h]
-        else:
-            flat[pl.ds(64, 4), :] = regs[0][:4]
+    joined = join_lines(got_ref, 0)
+    for c in range(4):
+        for h in range(2):
+            at = 16 * c + 8 * h
+            flat[pl.ds(32 * h + c, 8, stride=4), :] = joined[at : at + 8]
+    flat[pl.ds(64, 4), :] = joined[64:68]
 
 
 def edge_kernel(top_ref, bottom_ref, top_out_ref, bottom_out_ref):
@@ -551,19 +574,28 @@
     group_source = for_group(source)
     group_wall = for_group(wall_type[None])
 
-    packed = call(
+    any_place = pl.BlockSpec(memory_space=pl.ANY)
+    vmem = pl.BlockSpec(memory_space=pltpu.VMEM)
+    packed, couple_rows, rhs_rows = call(
         pack_kernel,
-        shape(GROUPS, TOTALROWS // 8, LANES),
-        [(40, LANES)],
-        (face_coef, face, cell, time_term.transpose(1, 0, 2), couple_rows, rhs_rows),
+        (shape(GROUPS, TOTALROWS // 8, LANES), shape(4 * WIDTH, 4, LANES), shape(WIDTH, 4, LANES)),
+        [
+            (4, LANES), (WIDTH * WIDTH, 4, LANES), (WIDTH * WIDTH, 4, LANES), (WIDTH, 4, LANES),
+            (SKEW_TILES, 4, LANES), (40, LANES), pltpu.SemaphoreType.DMA((6,)),
+        ],
+        [
+            pltpu.with_memory_space_constraint(a, pltpu.HBM)
+            for a in (face_coef, face, cell, time_term.transpose(1, 0, 2), couple_rows, rhs_rows)
+        ],
         20000000,
         "pack",
-    )
-    any_place = pl.BlockSpec(memory_space=pl.ANY)
+        in_specs=[pl.BlockSpec(memory_space=pltpu.HBM)] * 6,
+        out_specs=(vmem,) * 3,
+    )
     packed = call(
         right_kernel,
         shape(GROUPS, TOTALROWS // 8, LANES),
-        [(GROUPS, 16, LANES), pltpu.SemaphoreType.DMA(())],
+        [(GROUPS, COLS, LANES), pltpu.SemaphoreType.DMA(())],
         (start, low, high, index, kind, couple_rows, rhs_rows, packed),
         1000000,
         "right",
@@ -585,7 +617,8 @@
             shape(5 * VROWS, LANES),
         ),
         [
-            (TOTALROWS, LANES), (BELOWROWS, LANES), (2 * BROWS, LANES), (2 * DROWS, LANES),
+            (TOTALROWS // 4, 4, LANES), (WIDTH * WIDTH, 4, LANES), (WIDTH * WIDTH, 4, LANES),
+            (BELOWROWS, LANES), (2 * BROWS, LANES), (2 * DROWS, LANES),
             (BROWS, LANES), (BROWS, LANES), (24 * 4, LANES),
         ],
         (received, group_wall),
@@ -602,7 +635,7 @@
     high = lax.ppermute(bottom, "surf", down)
     sent = call(
         solve_kernel,
-        shape(GROUPS, 16, LANES),
+        shape(GROUPS, COLS, LANES),
         [(VROWS, LANES), (24 * 24, LANES)],
         (everyone, low, high, group_offset, group_source, vectors, inverses, blocks, held),
         3000000,

time: 97.4 us -> 77.3 us (0.79)
  Pallas kernels: 29.3 us -> 18.4 us
  local copies, waits for them, and re-layouts: 6.32 us -> 1.07 us
  blocking collectives: 46.3 us -> 43.3 us
    pallas_call x6, Pallas kernels: 29.3 us -> 18.4 us  [call(): pl.pallas_call(kernel, out_shape=outputs, scratch_shapes=[pltpu.VMEM(dims...]
    unnamed x14 -> x2, local copies, waits for them, and re-layouts: 5.25 us -> 0.01 us
    all_to_all x3, blocking collectives: 46.3 us -> 43.3 us  [across(): return lax.all_to_all(value, 'line', 0, 0, tiled=True)]
  transfers between devices with their start and end apart: 4 -> 4, of which waited for: 2 -> 2; matrix products, arithmetic and copies ran while one was open for 2% -> 2% of each run, Pallas kernels for 6% -> 2%
where the time goes in v2:
time: 77.3 us; the launch traced here: 77 us
  blocking collectives  43.3 us (56%)
  Pallas kernels  18.4 us (24%)
  starting transfers between devices  7.97 us (10%)
  waiting for transfers between devices  5.49 us (7%)
  local copies, waits for them, and re-layouts  1.07 us (1%)
    all_to_all x3, blocking collectives, across(): return lax.all_to_all(value, 'line', 0, 0, tiled=True)  43.3 us
    pallas_call x6, Pallas kernels, call(): pl.pallas_call(kernel, out_shape=outputs, scratch_shapes=[pltpu.VMEM(dims...  18.4 us
    ppermute x1, waiting for transfers between devices, on_device(): high = lax.ppermute(bottom, 'surf', down)  4.43 us
    ppermute x1, starting transfers between devices, on_device(): low = lax.ppermute(top, 'surf', up)  4.11 us
    ppermute x1, starting transfers between devices, on_device(): low = lax.ppermute(start, 'surf', up)  3.18 us
  transfers between devices with their start and end apart: 4, of which 2 were waited for; matrix products, arithmetic and copies ran while one was open for 2% of the time, Pallas kernels for 2%

profile of v2, /device:TPU:99, one launch (start us, length us, event | category | flops | bytes accessed | tf_op | source)
XLA Modules:
  0.0 77.0 jit_solution(15649185967522209912)
XLA Ops:
  0.0 0.0 copy-start
  0.0 0.7 collective-permute-start.1
  0.7 3.2 %collective-permute-start = (f32[17,4,128]{2,1,0:T(4,128)}, f32[17,4,128]{2,1,0:T(4,128)S(1)}, u32[]{:S(2)}, u32[]{:S(2)}) collective-permute-start(f32[17,4,128]{2,1,0:T(4,128)} %bitcast.14), channel_id=1, source_target_pairs={{0,1},{1,2},{2,3},{3,4},{4,5},{5,6},{6,7},{7,8},{8,9},{9,10},{10,1... | collective-permute-start | bytes 104456 | tf_op jit(solution)/shard_map/ppermute | solution.py:552
  3.9 0.7 fusion.4
  4.6 0.1 constant_dynamic-slice_fusion
  4.7 0.1 tile.13
  4.8 0.7 dynamic-slice.3
  5.5 0.1 tile.32.wall_ref
  5.6 0.1 tile.30.from_ref
  5.7 1.7 %pack.1 = (f32[8,288,128]{2,1,0:T(8,128)S(1)}, f32[68,4,128]{2,1,0:T(4,128)S(1)}, f32[17,4,128]{2,1,0:T(4,128)S(1)}) custom-call(f32[4,128]{1,0:T(4,128)} %coef_in.1, f32[289,4,128]{2,1,0:T(4,128)} %bitcast.16, f32[289,4,128]{2,1,0:T(4,128)} %bitcast.17, f32[17,4,128]{2,1,0:T(4,128)} %bitcast.19, f32[68,4,128]{2,1,0:T(4,128)} %bitcast.18, f32[17,4,128]{2,1,0:T(4,128)} %bitcast.20), custom_call_target="tpu_custom_call" | custom-call | flops 20000000 | bytes 1000000 | tf_op jit(solution)/shard_map/pack/pallas_call | solution.py:525
  7.4 0.0 collective-permute-done.1.high_ref
  7.4 0.0 collective-permute-done.low_ref
  7.4 0.0 copy-done
  7.4 0.4 right.1
  7.8 22.6 %all_to_all.15.got_ref = f32[8,288,128]{2,1,0:T(8,128)S(1)} all-to-all(f32[8,288,128]{2,1,0:T(8,128)S(1)} %right.1), channel_id=1, replica_groups=mesh['line'=8,'surf'=32] {'line'}, dimensions={0} | all-to-all | bytes 2359296 | tf_op jit(solution)/shard_map/all_to_all | solution.py:537
  30.4 13.9 %factor.1 = (f32[8,72,128]{2,1,0:T(8,128)S(1)}, f32[2856,128]{1,0:T(8,128)S(1)}, f32[4080,128]{1,0:T(8,128)S(1)}, f32[2040,128]{1,0:T(8,128)S(1)}, f32[360,128]{1,0:T(8,128)S(1)}) custom-call(f32[8,288,128]{2,1,0:T(8,128)S(1)} %all_to_all.15.got_ref, s32[1,128]{1,0:T(1,128)S(1)} %tile.32.wall_ref), custom_call_target="tpu_custom_call" | custom-call | flops 30000000 | bytes 1000000 | tf_op jit(solution)/shard_map/factor/pallas_call | solution.py:525
  44.3 11.6 %all_to_all.16.top_ref.bottom_ref.all_ref = f32[8,72,128]{2,1,0:T(8,128)S(1)} all-to-all(f32[8,72,128]{2,1,0:T(8,128)S(1)} %get-tuple-element.24), channel_id=1, replica_groups=mesh['line'=8,'surf'=32] {'line'}, dimensions={0} | all-to-all | bytes 589824 | tf_op jit(solution)/shard_map/all_to_all | solution.py:537
  55.9 4.1 %collective-permute-start.2 = (f32[72,128]{1,0:T(8,128)S(1)}, f32[72,128]{1,0:T(8,128)S(1)}, u32[]{:S(2)}, u32[]{:S(2)}) collective-permute-start(f32[72,128]{1,0:T(8,128)S(1)} %get-tuple-element.25), channel_id=1, source_target_pairs={{0,1},{1,2},{2,3},{3,4},{4,5},{5,6},{6,7},{7,8},{8,9},{9,10},{10,1... | collective-permute-start | bytes 110600 | tf_op jit(solution)/shard_map/ppermute | solution.py:634
  60.0 0.0 collective-permute-start.3
  60.0 1.1 %collective-permute-done.2.low_ref = f32[72,128]{1,0:T(8,128)S(1)} collective-permute-done((f32[72,128]{1,0:T(8,128)S(1)}, f32[72,128]{1,0:T(8,128)S(1)}, u32[]{:S(2)}, u32[]{:S(2)}) %collective-permute-start.2) | collective-permute-done | bytes 36896 | tf_op jit(solution)/shard_map/ppermute | solution.py:634
  61.1 4.4 %collective-permute-done.3.high_ref = f32[72,128]{1,0:T(8,128)S(1)} collective-permute-done((f32[72,128]{1,0:T(8,128)S(1)}, f32[72,128]{1,0:T(8,128)S(1)}, u32[]{:S(2)}, u32[]{:S(2)}) %collective-permute-start.3) | collective-permute-done | bytes 36896 | tf_op jit(solution)/shard_map/ppermute | solution.py:635
  65.5 1.7 %solve.1 = f32[8,16,128]{2,1,0:T(8,128)S(1)} custom-call(f32[8,72,128]{2,1,0:T(8,128)S(1)} %all_to_all.16.top_ref.bottom_ref.all_ref, f32[72,128]{1,0:T(8,128)S(1)} %collective-permute-done.2.low_ref, f32[72,128]{1,0:T(8,128)S(1)} %collective-permute-done.3.high_ref, s32[4,128]{1,0:T(4,128)S(1)} %broadcast_add_fusion.index_ref, s32[4,128]{1,0:T(4,128)S(1)} %tile.30.from_ref, ...), custom_call_target="tpu_custom_call" | custom-call | flops 3000000 | bytes 1000000 | tf_op jit(solution)/shard_map/solve/pallas_call | solution.py:525
  67.3 9.1 %all_to_all.17.got_ref = f32[8,16,128]{2,1,0:T(8,128)S(1)} all-to-all(f32[8,16,128]{2,1,0:T(8,128)S(1)} %solve.1), channel_id=1, replica_groups=mesh['line'=8,'surf'=32] {'line'}, dimensions={0} | all-to-all | bytes 131072 | tf_op jit(solution)/shard_map/all_to_all | solution.py:537
  76.3 0.7 unpack.1
  (7 shorter events, 0.0 us)
Async XLA Ops:
  0.0 7.4 %copy-start = (f32[4,17,128]{2,0,1:T(4,128)S(1)}, f32[4,17,128]{2,0,1:T(4,128)}, u32[]{:S(2)}) copy-start(f32[4,17,128]{2,0,1:T(4,128)} %param.15) | copy-start | bytes 104452
  0.0 7.4 %collective-permute-start.1 = (f32[17,4,128]{2,1,0:T(4,128)}, f32[17,4,128]{2,1,0:T(4,128)S(1)}, u32[]{:S(2)}, u32[]{:S(2)}) collective-permute-start(f32[17,4,128]{2,1,0:T(4,128)} %bitcast.13), channel_id=1, source_target_pairs={{1,0},{2,1},{3,2},{4,3},{5,4},{6,5},{7,6},{8,7},{9,8},{10,9},{11,1... | collective-permute-start | bytes 104456 | tf_op jit(solution)/shard_map/ppermute | solution.py:553
  0.7 6.7 %collective-permute-start = (f32[17,4,128]{2,1,0:T(4,128)}, f32[17,4,128]{2,1,0:T(4,128)S(1)}, u32[]{:S(2)}, u32[]{:S(2)}) collective-permute-start(f32[17,4,128]{2,1,0:T(4,128)} %bitcast.14), channel_id=1, source_target_pairs={{0,1},{1,2},{2,3},{3,4},{4,5},{5,6},{6,7},{7,8},{8,9},{9,10},{10,1... | collective-permute-start | bytes 104456 | tf_op jit(solution)/shard_map/ppermute | solution.py:552
  55.9 5.2 %collective-permute-start.2 = (f32[72,128]{1,0:T(8,128)S(1)}, f32[72,128]{1,0:T(8,128)S(1)}, u32[]{:S(2)}, u32[]{:S(2)}) collective-permute-start(f32[72,128]{1,0:T(8,128)S(1)} %get-tuple-element.25), channel_id=1, source_target_pairs={{0,1},{1,2},{2,3},{3,4},{4,5},{5,6},{6,7},{7,8},{8,9},{9,10},{10,1... | collective-permute-start | bytes 110600 | tf_op jit(solution)/shard_map/ppermute | solution.py:634
  60.0 5.5 %collective-permute-start.3 = (f32[72,128]{1,0:T(8,128)S(1)}, f32[72,128]{1,0:T(8,128)S(1)}, u32[]{:S(2)}, u32[]{:S(2)}) collective-permute-start(f32[72,128]{1,0:T(8,128)S(1)} %get-tuple-element.26), channel_id=1, source_target_pairs={{1,0},{2,1},{3,2},{4,3},{5,4},{6,5},{7,6},{8,7},{9,8},{10,9},{11,1... | collective-permute-start | bytes 110600 | tf_op jit(solution)/shard_map/ppermute | solution.py:635

commit v3 on v2

--- a/solution.py
+++ b/solution.py
@@ -13,6 +13,7 @@
 BROWS = 40 * WIDTH
 BELOWROWS = 296
 VROWS = 72
+UNROLL = True
 MATRIX_BLOCKS = 17
 TOTALROWS = 128 * (MATRIX_BLOCKS + 1)
 SKEW_TILES = WIDTH * (WIDTH - 1) // 2
@@ -170,7 +171,7 @@
 
 
 def by_rows(step):
-    lax.fori_loop(0, WIDTH // 2, lambda t, _: step([2 * t, 2 * t + 1]), 0)
+    lax.fori_loop(0, WIDTH // 2, lambda t, _: step([2 * t, 2 * t + 1]), 0, unroll=UNROLL)
     step([WIDTH - 1])
 
 
@@ -178,7 +179,7 @@
     return term if total is None else total + term
 
 
-def normalise(inverse, inverse_base, source, source_base, result, result_base):
+def normalise(inverse, inverse_base, source, source_base, result, result_base, shifted=None, steps=0):
     def step(rows):
         starts = [pl.multiple_of(24 * i, 8) for i in rows]
         sums = [[None] * 5 for _ in rows]
@@ -192,6 +193,8 @@
             to = pl.multiple_of(40 * i, 8)
             for v in range(5):
                 result[pl.ds(result_base + to + 8 * v, 8), :] = sums[r][v]
+                if shifted is not None:
+                    shifted[pl.ds(to + 8 * v, 8), :] = pltpu.roll(sums[r][v], (COLS * steps) % LANES, 1)
         return 0
 
     by_rows(step)
@@ -228,6 +231,36 @@
                 )
             new_diag[pl.ds(new_diag_base + to + 16, 8), :] = (
                 tile(diag, diag_base + to + 16) - pltpu.roll(first[4], 7, 0) - second[4]
+            )
+        return 0
+
+    by_rows(step)
+
+
+def finish(blocks, base, diag, diag_base, low, high, value_ref, new_diag, new_diag_base):
+    def step(rows):
+        starts = [pl.multiple_of(40 * i, 8) for i in rows]
+        sums = [[None] * 2 for _ in rows]
+        ends = [[None] * 2 for _ in rows]
+        for j in range(WIDTH):
+            below = [row(blocks, base + at + left_at(j)) for at in starts]
+            above = [row(blocks, base + at + right_at(j)) for at in starts]
+            for v in range(2):
+                first, second = tile(low, 40 * j + 16 + 8 * v), tile(high, 40 * j + 8 * v)
+                for r in range(len(rows)):
+                    sums[r][v] = plus(sums[r][v], below[r] * first + above[r] * second)
+            first, second = tile(low, 40 * j + 32), tile(high, 40 * j + 32)
+            for r in range(len(rows)):
+                ends[r][0] = plus(ends[r][0], below[r] * first)
+                ends[r][1] = plus(ends[r][1], above[r] * second)
+        for r, (at, i) in enumerate(zip(starts, rows)):
+            first, second = ends[r]
+            value_ref[pl.ds(at, 8), :] = tile(blocks, base + at + 32) - first - second
+            to = pl.multiple_of(24 * i, 8)
+            for v in range(2):
+                new_diag[pl.ds(new_diag_base + to + 8 * v, 8), :] = tile(diag, diag_base + to + 8 * v) - sums[r][v]
+            new_diag[pl.ds(new_diag_base + to + 16, 8), :] = (
+                tile(diag, diag_base + to + 16) - pltpu.roll(first, 7, 0) - second
             )
         return 0
 
@@ -399,7 +432,7 @@
     build(1, blocks_ref, 0, work_diag, 0)
     build(3, blocks_ref, B, work_diag, D)
     invert_in_place([(inverse_ref, 0), (inverse_ref, D)])
-    normalise(inverse_ref, 0, work_blocks, 0, held_ref, 0)
+    normalise(inverse_ref, 0, work_blocks, 0, held_ref, 0, high, -1)
     normalise(inverse_ref, D, work_blocks, B, held_ref, B)
 
     def turn(source, source_base, result, steps):
@@ -408,12 +441,10 @@
                 tile(source, source_base + 8 * t), (COLS * steps) % LANES, 1
             )
 
-    turn(held_ref, 0, high, -1)
     eliminate(blocks_ref, 0, work_diag, 0, held_ref, 0, held_ref, B, work_blocks, 0, inverse_ref, 2 * D)
     eliminate(blocks_ref, B, work_diag, D, held_ref, B, high, 0, blocks_ref, 2 * B, work_diag, 0)
     invert_in_place([(inverse_ref, 2 * D)])
-    normalise(inverse_ref, 2 * D, work_blocks, 0, held_ref, 2 * B)
-    turn(held_ref, 2 * B, high, -1)
+    normalise(inverse_ref, 2 * D, work_blocks, 0, held_ref, 2 * B, high, -1)
     eliminate(
         blocks_ref, 2 * B, work_diag, 0, held_ref, 2 * B, high, 0, blocks_ref, 3 * B, inverse_ref, 3 * D
     )
@@ -421,19 +452,18 @@
         source = 3 + k
         work_diag[pl.ds(0, D), :] = inverse_ref[pl.ds(source * D, D), :]
         invert_in_place([(inverse_ref, source * D)])
-        normalise(inverse_ref, source * D, blocks_ref, source * B, work_blocks, 0)
-        turn(work_blocks, 0, low, 2**k)
-        turn(work_blocks, 0, high, -(2**k))
+        normalise(inverse_ref, source * D, blocks_ref, source * B, work_blocks, 0, low, 2**k)
         if k < 2:
-            new, new_base = blocks_ref, (source + 1) * B
+            turn(work_blocks, 0, high, -(2**k))
+            eliminate(
+                blocks_ref, source * B, work_diag, 0, low, 0, high, 0, blocks_ref, (source + 1) * B,
+                inverse_ref, (source + 1) * D,
+            )
         else:
-            new, new_base = work_blocks, B
-        eliminate(
-            blocks_ref, source * B, work_diag, 0, low, 0, high, 0, new, new_base, inverse_ref, (source + 1) * D
-        )
+            finish(blocks_ref, source * B, work_diag, 0, low, low, high, inverse_ref, (source + 1) * D)
     invert_in_place([(inverse_ref, 6 * D)])
     scratch = Scratch(scratch_ref)
-    last = matvec(inverse_ref, 6 * D, 24, plain, lambda j: row(work_blocks, B + 40 * j + 34))
+    last = matvec(inverse_ref, 6 * D, 24, plain, lambda j: row(high, 40 * j + 2))
     forward = []
     for index in range(3):
         base = index * B

time: 77.3 us -> 75 us (0.970)
  Pallas kernels: 18.4 us -> 16.1 us
    pallas_call x6, Pallas kernels: 18.4 us -> 16.1 us  [call(): pl.pallas_call(kernel, out_shape=outputs, scratch_shapes=[pltpu.VMEM(dims...]
where the time goes in v3:
time: 75 us; the launch traced here: 74.7 us
  blocking collectives  43.3 us (58%)
  Pallas kernels  16.1 us (21%)
  starting transfers between devices  7.97 us (11%)
  waiting for transfers between devices  5.49 us (7%)
  local copies, waits for them, and re-layouts  1.07 us (1%)
    all_to_all x3, blocking collectives, across(): return lax.all_to_all(value, 'line', 0, 0, tiled=True)  43.3 us
    pallas_call x6, Pallas kernels, call(): pl.pallas_call(kernel, out_shape=outputs, scratch_shapes=[pltpu.VMEM(dims...  16.1 us
    ppermute x1, waiting for transfers between devices, on_device(): high = lax.ppermute(bottom, 'surf', down)  4.43 us
    ppermute x1, starting transfers between devices, on_device(): low = lax.ppermute(top, 'surf', up)  4.11 us
    ppermute x1, starting transfers between devices, on_device(): low = lax.ppermute(start, 'surf', up)  3.18 us
  transfers between devices with their start and end apart: 4, of which 2 were waited for; matrix products, arithmetic and copies ran while one was open for 2% of the time, Pallas kernels for 2%

profile of v3, /device:TPU:99, one launch (start us, length us, event | category | flops | bytes accessed | tf_op | source)
XLA Modules:
  0.0 74.7 jit_solution(3750722876802415993)
XLA Ops:
  0.0 0.0 copy-start
  0.0 0.7 collective-permute-start.1
  0.7 3.2 %collective-permute-start = (f32[17,4,128]{2,1,0:T(4,128)}, f32[17,4,128]{2,1,0:T(4,128)S(1)}, u32[]{:S(2)}, u32[]{:S(2)}) collective-permute-start(f32[17,4,128]{2,1,0:T(4,128)} %bitcast.14), channel_id=1, source_target_pairs={{0,1},{1,2},{2,3},{3,4},{4,5},{5,6},{6,7},{7,8},{8,9},{9,10},{10,1... | collective-permute-start | bytes 104456 | tf_op jit(solution)/shard_map/ppermute | solution.py:582
  3.9 0.7 fusion.4
  4.6 0.1 constant_dynamic-slice_fusion
  4.7 0.1 tile.13
  4.8 0.7 dynamic-slice.3
  5.5 0.1 tile.32.wall_ref
  5.6 0.1 tile.30.from_ref
  5.7 1.7 %pack.1 = (f32[8,288,128]{2,1,0:T(8,128)S(1)}, f32[68,4,128]{2,1,0:T(4,128)S(1)}, f32[17,4,128]{2,1,0:T(4,128)S(1)}) custom-call(f32[4,128]{1,0:T(4,128)} %coef_in.1, f32[289,4,128]{2,1,0:T(4,128)} %bitcast.16, f32[289,4,128]{2,1,0:T(4,128)} %bitcast.17, f32[17,4,128]{2,1,0:T(4,128)} %bitcast.19, f32[68,4,128]{2,1,0:T(4,128)} %bitcast.18, f32[17,4,128]{2,1,0:T(4,128)} %bitcast.20), custom_call_target="tpu_custom_call" | custom-call | flops 20000000 | bytes 1000000 | tf_op jit(solution)/shard_map/pack/pallas_call | solution.py:555
  7.4 0.0 collective-permute-done.1.high_ref
  7.4 0.0 collective-permute-done.low_ref
  7.4 0.0 copy-done
  7.4 0.4 right.1
  7.8 22.6 %all_to_all.15.got_ref = f32[8,288,128]{2,1,0:T(8,128)S(1)} all-to-all(f32[8,288,128]{2,1,0:T(8,128)S(1)} %right.1), channel_id=1, replica_groups=mesh['line'=8,'surf'=32] {'line'}, dimensions={0} | all-to-all | bytes 2359296 | tf_op jit(solution)/shard_map/all_to_all | solution.py:567
  30.4 11.5 %factor.1 = (f32[8,72,128]{2,1,0:T(8,128)S(1)}, f32[2856,128]{1,0:T(8,128)S(1)}, f32[4080,128]{1,0:T(8,128)S(1)}, f32[2040,128]{1,0:T(8,128)S(1)}, f32[360,128]{1,0:T(8,128)S(1)}) custom-call(f32[8,288,128]{2,1,0:T(8,128)S(1)} %all_to_all.15.got_ref, s32[1,128]{1,0:T(1,128)S(1)} %tile.32.wall_ref), custom_call_target="tpu_custom_call" | custom-call | flops 30000000 | bytes 1000000 | tf_op jit(solution)/shard_map/factor/pallas_call | solution.py:555
  42.0 11.6 %all_to_all.16.top_ref.bottom_ref.all_ref = f32[8,72,128]{2,1,0:T(8,128)S(1)} all-to-all(f32[8,72,128]{2,1,0:T(8,128)S(1)} %get-tuple-element.24), channel_id=1, replica_groups=mesh['line'=8,'surf'=32] {'line'}, dimensions={0} | all-to-all | bytes 589824 | tf_op jit(solution)/shard_map/all_to_all | solution.py:567
  53.6 4.1 %collective-permute-start.2 = (f32[72,128]{1,0:T(8,128)S(1)}, f32[72,128]{1,0:T(8,128)S(1)}, u32[]{:S(2)}, u32[]{:S(2)}) collective-permute-start(f32[72,128]{1,0:T(8,128)S(1)} %get-tuple-element.25), channel_id=1, source_target_pairs={{0,1},{1,2},{2,3},{3,4},{4,5},{5,6},{6,7},{7,8},{8,9},{9,10},{10,1... | collective-permute-start | bytes 110600 | tf_op jit(solution)/shard_map/ppermute | solution.py:664
  57.7 0.0 collective-permute-start.3
  57.7 1.1 %collective-permute-done.2.low_ref = f32[72,128]{1,0:T(8,128)S(1)} collective-permute-done((f32[72,128]{1,0:T(8,128)S(1)}, f32[72,128]{1,0:T(8,128)S(1)}, u32[]{:S(2)}, u32[]{:S(2)}) %collective-permute-start.2) | collective-permute-done | bytes 36896 | tf_op jit(solution)/shard_map/ppermute | solution.py:664
  58.8 4.4 %collective-permute-done.3.high_ref = f32[72,128]{1,0:T(8,128)S(1)} collective-permute-done((f32[72,128]{1,0:T(8,128)S(1)}, f32[72,128]{1,0:T(8,128)S(1)}, u32[]{:S(2)}, u32[]{:S(2)}) %collective-permute-start.3) | collective-permute-done | bytes 36896 | tf_op jit(solution)/shard_map/ppermute | solution.py:665
  63.2 1.7 %solve.1 = f32[8,16,128]{2,1,0:T(8,128)S(1)} custom-call(f32[8,72,128]{2,1,0:T(8,128)S(1)} %all_to_all.16.top_ref.bottom_ref.all_ref, f32[72,128]{1,0:T(8,128)S(1)} %collective-permute-done.2.low_ref, f32[72,128]{1,0:T(8,128)S(1)} %collective-permute-done.3.high_ref, s32[4,128]{1,0:T(4,128)S(1)} %broadcast_add_fusion.index_ref, s32[4,128]{1,0:T(4,128)S(1)} %tile.30.from_ref, ...), custom_call_target="tpu_custom_call" | custom-call | flops 3000000 | bytes 1000000 | tf_op jit(solution)/shard_map/solve/pallas_call | solution.py:555
  64.9 9.1 %all_to_all.17.got_ref = f32[8,16,128]{2,1,0:T(8,128)S(1)} all-to-all(f32[8,16,128]{2,1,0:T(8,128)S(1)} %solve.1), channel_id=1, replica_groups=mesh['line'=8,'surf'=32] {'line'}, dimensions={0} | all-to-all | bytes 131072 | tf_op jit(solution)/shard_map/all_to_all | solution.py:567
  74.0 0.7 unpack.1
  (7 shorter events, 0.0 us)
Async XLA Ops:
  0.0 7.4 %copy-start = (f32[4,17,128]{2,0,1:T(4,128)S(1)}, f32[4,17,128]{2,0,1:T(4,128)}, u32[]{:S(2)}) copy-start(f32[4,17,128]{2,0,1:T(4,128)} %param.15) | copy-start | bytes 104452
  0.0 7.4 %collective-permute-start.1 = (f32[17,4,128]{2,1,0:T(4,128)}, f32[17,4,128]{2,1,0:T(4,128)S(1)}, u32[]{:S(2)}, u32[]{:S(2)}) collective-permute-start(f32[17,4,128]{2,1,0:T(4,128)} %bitcast.13), channel_id=1, source_target_pairs={{1,0},{2,1},{3,2},{4,3},{5,4},{6,5},{7,6},{8,7},{9,8},{10,9},{11,1... | collective-permute-start | bytes 104456 | tf_op jit(solution)/shard_map/ppermute | solution.py:583
  0.7 6.7 %collective-permute-start = (f32[17,4,128]{2,1,0:T(4,128)}, f32[17,4,128]{2,1,0:T(4,128)S(1)}, u32[]{:S(2)}, u32[]{:S(2)}) collective-permute-start(f32[17,4,128]{2,1,0:T(4,128)} %bitcast.14), channel_id=1, source_target_pairs={{0,1},{1,2},{2,3},{3,4},{4,5},{5,6},{6,7},{7,8},{8,9},{9,10},{10,1... | collective-permute-start | bytes 104456 | tf_op jit(solution)/shard_map/ppermute | solution.py:582
  53.6 5.2 %collective-permute-start.2 = (f32[72,128]{1,0:T(8,128)S(1)}, f32[72,128]{1,0:T(8,128)S(1)}, u32[]{:S(2)}, u32[]{:S(2)}) collective-permute-start(f32[72,128]{1,0:T(8,128)S(1)} %get-tuple-element.25), channel_id=1, source_target_pairs={{0,1},{1,2},{2,3},{3,4},{4,5},{5,6},{6,7},{7,8},{8,9},{9,10},{10,1... | collective-permute-start | bytes 110600 | tf_op jit(solution)/shard_map/ppermute | solution.py:664
  57.7 5.5 %collective-permute-start.3 = (f32[72,128]{1,0:T(8,128)S(1)}, f32[72,128]{1,0:T(8,128)S(1)}, u32[]{:S(2)}, u32[]{:S(2)}) collective-permute-start(f32[72,128]{1,0:T(8,128)S(1)} %get-tuple-element.26), channel_id=1, source_target_pairs={{1,0},{2,1},{3,2},{4,3},{5,4},{6,5},{7,6},{8,7},{9,8},{10,9},{11,1... | collective-permute-start | bytes 110600 | tf_op jit(solution)/shard_map/ppermute | solution.py:665
